TPU v7x, 128 devices: a whole 4x4x4 slice. The times are simulated.
128 devices in a mesh: dp: 64 (over z, y, x), tensor: 2 (over core).
Axes of the slice: x: 4, y: 4, z: 4, core: 2. Of those that a mesh axis runs over, the one named last changes fastest.
Arguments:
- current: float32 [128, 4096], P('dp'), may hold values from -6 to 6
- noise_draw: float32 [128, 4096], P('dp'), may hold values from -6 to 6
- labels: bfloat16 [128, 1152], P('dp'), may hold values from -6 to 6
- time_now: float32 [128], P('dp'), may hold values from 0.4 to 1
- step_size: float32 [128], P('dp'), may hold values from 0.005 to 0.02
- accept: int32 [128], P('dp'), may hold values 0 or 1
- patch_weight: bfloat16 [16, 1152], replicated, may hold values from -1.5 to 1.5
- time_in: bfloat16 [256, 1152], replicated, may hold values from -0.375 to 0.375
- time_out: bfloat16 [1152, 1152], replicated, may hold values from -0.1875 to 0.1875
- qkv_weight: bfloat16 [1, 1152, 3, 1152], P(None, None, None, 'tensor'), may hold values from -1 to 1
- out_weight: bfloat16 [1, 1152, 1152], P(None, None, 'tensor'), may hold values from -0.1875 to 0.1875
- ada_weight: bfloat16 [1, 1152, 3456], P(None, 'dp', 'tensor'), may hold values from -0.1875 to 0.1875
- final_ada: bfloat16 [1152, 2304], P('dp', 'tensor'), may hold values from -0.1875 to 0.1875
- final_proj: bfloat16 [1152, 16], replicated, may hold values from -0.1875 to 0.1875
Outputs:
- next_state: float32 [128, 4096], P('dp')
- error_norm: float32 [128], P('dp')
All inputs are finite; a program needn't handle non-finite values. No bound on the sum of `accept` on one device may be relied on, other than what follows from the above.
Results may differ from a plain program's by a relative error of at most 0.015.
Values may be sent and summed in bfloat16 or wider, within the bound.
A program may use at most 128 MiB of HBM per device.

v0:
```python
import math

import jax
import jax.numpy as jnp
from jax import lax
from jax.sharding import PartitionSpec as P

D = 1152
PATCH_VALS = 16
HEAD_DIM = 72


beta_low = 0.1
beta_high = 20.0
tol_abs = 0.0078
tol_rel = 0.05
norm_eps = 1e-06


def from_everyone(array, axis):
    peers = lax.axis_size(axis)
    return lax.all_to_all(
        jnp.broadcast_to(array[None], (peers, *array.shape)), axis, 0, 0, tiled=True
    )


def of_everyone(array, axis):
    return from_everyone(array, axis).astype(jnp.float32).sum(axis=0)


def beta_at(moments):
    return beta_low + (beta_high - beta_low) * moments


def sigma_at(moments):
    integral = beta_low * moments + 0.5 * (beta_high - beta_low) * moments * moments
    return jnp.sqrt(1.0 - jnp.exp(-integral))


def time_features(moments, feature_count):
    half_count = feature_count // 2
    freq_index = jnp.arange(half_count, dtype=jnp.float32)
    freq_rates = jnp.exp(-math.log(10000.0) * freq_index / half_count)
    angles = 1000.0 * moments[:, None] * freq_rates[None, :]
    return jnp.concatenate([jnp.cos(angles), jnp.sin(angles)], axis=1)


def position_table(positions, feature_count):
    half_count = feature_count // 2
    freq_index = jnp.arange(half_count, dtype=jnp.float32)
    freq_rates = jnp.exp(-math.log(10000.0) * freq_index / half_count)
    angles = positions.astype(jnp.float32)[:, None] * freq_rates[None, :]
    return jnp.concatenate([jnp.sin(angles), jnp.cos(angles)], axis=1)


def condition(moments, labels, time_in, time_out):
    features = time_features(moments, time_in.shape[0]).astype(jnp.bfloat16)
    hidden = jax.nn.silu(jnp.dot(features, time_in, preferred_element_type=jnp.float32)).astype(
        jnp.bfloat16
    )
    joined = labels.astype(jnp.float32) + jnp.dot(
        hidden, time_out, preferred_element_type=jnp.float32
    )
    return jax.nn.silu(joined).astype(jnp.bfloat16)


def layer_norm(values):
    average = jnp.mean(values, axis=-1, keepdims=True)
    centred = values - average
    spread_sq = jnp.mean(centred * centred, axis=-1, keepdims=True)
    return centred * lax.rsqrt(spread_sq + norm_eps)


def modulate(values, shift_vec, scale_vec):
    return (layer_norm(values) * (1.0 + scale_vec[:, None]) + shift_vec[:, None]).astype(
        jnp.bfloat16
    )


def drift(values, moments, noise_guess):
    beta_rate = beta_at(moments)[:, None]
    return 0.5 * beta_rate * values - beta_rate * noise_guess / sigma_at(moments)[:, None]


def attend(projected, head_dim):
    lat_count, token_count, _, feature_width = projected.shape
    head_count = feature_width // head_dim
    shaped = projected.reshape(lat_count, token_count, 3, head_count, head_dim)
    scores = jnp.einsum(
        "lqhe,lkhe->lhqk", shaped[:, :, 0], shaped[:, :, 1], preferred_element_type=jnp.float32
    ) * head_dim ** (-0.5)
    attn_probs = jax.nn.softmax(scores, axis=-1).astype(jnp.bfloat16)
    mixture = jnp.einsum(
        "lhqk,lkhe->lqhe", attn_probs, shaped[:, :, 2], preferred_element_type=jnp.float32
    )
    return mixture.astype(jnp.bfloat16).reshape(lat_count, token_count, feature_width)


def shards(
    current,
    noise_draw,
    labels,
    time_now,
    step_size,
    accept,
    patch_weight,
    time_in,
    time_out,
    qkv_weight,
    out_weight,
    ada_weight,
    final_ada,
    final_proj,
):
    lat_count = current.shape[0]
    tok_count = current.shape[1] // PATCH_VALS
    layer_total = ada_weight.shape[0]
    layer_cols = ada_weight.shape[2]
    final_cols = final_ada.shape[1]
    tensor_size = lax.axis_size("tensor")
    later_time = time_now - step_size
    moments = jnp.concatenate([time_now, later_time])
    cond_act = condition(moments, jnp.concatenate([labels, labels], axis=0), time_in, time_out)
    own_rows = ada_weight.shape[1]
    packed = jnp.concatenate(
        [ada_weight.transpose(1, 0, 2).reshape(own_rows, layer_total * layer_cols), final_ada],
        axis=1,
    )
    row_total = cond_act.shape[0]
    packed_width = packed.shape[1]
    mod_local = jnp.dot(
        cond_act,
        lax.all_gather(packed, "dp", axis=0, tiled=True),
        preferred_element_type=jnp.float32,
    )
    gathered = lax.all_gather(mod_local.astype(jnp.bfloat16), "tensor", axis=1, tiled=True).astype(
        mod_local.dtype
    )
    arranged = gathered.reshape(row_total, tensor_size, packed_width)
    layer_mods = arranged[:, :, : layer_total * layer_cols].reshape(
        row_total, tensor_size, layer_total, layer_cols
    )
    layer_mods = layer_mods.transpose(0, 2, 1, 3).reshape(
        row_total, layer_total, tensor_size * layer_cols
    )
    final_mods = arranged[:, :, layer_total * layer_cols :].reshape(
        row_total, tensor_size * final_cols
    )
    positions = position_table(jnp.arange(tok_count, dtype=jnp.int32), D)

    def evaluate(latents, mod_rows, final_rows):
        tokens = latents.reshape(lat_count, tok_count, PATCH_VALS).astype(jnp.bfloat16)
        stream = (
            jnp.einsum("ltc,cd->ltd", tokens, patch_weight, preferred_element_type=jnp.float32)
            + positions[None]
        )
        shift_attn, scale_attn, gate_attn = jnp.split(mod_rows[:, 0], 3, axis=1)
        attn_in = modulate(stream, shift_attn, scale_attn)
        projected = jnp.einsum(
            "ltd,dck->ltck", attn_in, qkv_weight[0], preferred_element_type=jnp.float32
        ).astype(jnp.bfloat16)
        attended = attend(projected, HEAD_DIM)
        partial_value = jnp.einsum(
            "ltk,dk->ltd", attended, out_weight[0], preferred_element_type=jnp.float32
        )
        attn_sum = of_everyone(partial_value.astype(jnp.bfloat16), "tensor").astype(jnp.float32)
        stream = stream + gate_attn[:, None] * attn_sum
        shift_final, scale_final = jnp.split(final_rows, 2, axis=1)
        final_in = modulate(stream, shift_final, scale_final)
        guessed = jnp.einsum(
            "ltd,dc->ltc", final_in, final_proj, preferred_element_type=jnp.float32
        )
        return guessed.reshape(lat_count, tok_count * PATCH_VALS)

    noise_now = evaluate(current, layer_mods[:lat_count], final_mods[:lat_count])
    drift_now = drift(current, time_now, noise_now)
    spread = jnp.sqrt(step_size * beta_at(time_now))[:, None] * noise_draw
    euler_state = current + step_size[:, None] * drift_now + spread
    noise_later = evaluate(euler_state, layer_mods[lat_count:], final_mods[lat_count:])
    drift_later = drift(euler_state, later_time, noise_later)
    heun_state = current + 0.5 * step_size[:, None] * (drift_now + drift_later) + spread
    scale_ref = jnp.maximum(tol_abs, tol_rel * jnp.maximum(jnp.abs(heun_state), jnp.abs(current)))
    scaled_gap = (euler_state - heun_state) / scale_ref
    error_norm = jnp.sqrt(jnp.sum(scaled_gap * scaled_gap, axis=1) / current.shape[1])
    next_state = jnp.where(accept[:, None] == 1, heun_state, current)
    return (next_state, error_norm)


def solution(mesh):
    in_specs = (
        P("dp", None),
        P("dp", None),
        P("dp", None),
        P("dp"),
        P("dp"),
        P("dp"),
        P(),
        P(),
        P(),
        P(None, None, None, "tensor"),
        P(None, None, "tensor"),
        P(None, "dp", "tensor"),
        P("dp", "tensor"),
        P(),
    )
    out_specs = (P("dp", None), P("dp"))
    return jax.shard_map(shards, mesh=mesh, in_specs=in_specs, out_specs=out_specs, check_vma=False)
```

profile of v0, /device:TPU:1, one launch (start us, length us, event | category | flops | bytes accessed | tf_op | source)
XLA Modules:
  0.0 162.8 jit_solution(1953090648457118049)
XLA Ops:
  7.2 0.0 copy-start
  7.2 0.0 all-gather.4.cloned.1.call-start
  7.2 1.8 %maximum_bitcast_fusion = bf16[1,18,2880]{2,1,0:T(8,128)(2,1)} fusion(bf16[18,1152]{1,0:T(8,128)(2,1)} %param.26, bf16[18,1728]{1,0:T(8,128)(2,1)} %bitcast.106), kind=kLoop, calls=%fused_computation.66 | loop fusion | flops 207360 | bytes 207360
  9.0 0.0 all-gather.4.cloned.1.call-update
  9.1 0.8 convert_element_type.83
  9.8 0.1 convert_element_type.84
  10.0 0.7 broadcast_multiply_fusion.4
  10.7 0.7 maximum_multiply_fusion
  11.4 2.3 %multiply_sine_fusion = (f32[256,576]{1,0:T(8,128)S(1)}, f32[256,576]{1,0:T(8,128)S(1)}) fusion(f32[576]{0:T(1024)S(1)} %multiply_exponential_fusion, f32[256]{0:T(256)S(1)} %iota_convert_fusion), kind=kLoop, calls=%fused_computation.57 | loop fusion | flops 147456 | bytes 1182976 | tf_op jit(solution)/shard_map/sin | solution.py:53
  13.8 0.2 pad_maximum_fusion
  14.1 1.0 copy-done.4
  15.1 0.5 fusion.78
  15.6 1.4 copy-done.2
  17.0 0.4 multiply_reduce_fusion.5
  17.4 0.1 fusion.58
  17.5 0.2 fusion.60
  17.7 76.3 %all-gather.4.cloned.1.call-done = bf16[64,18,2880]{2,1,0:T(8,128)(2,1)} async-done(((bf16[1,18,2880]{2,1,0:T(8,128)(2,1)}), bf16[64,18,2880]{2,1,0:T(8,128)(2,1)}) %all-gather.4.cloned.1.call-update) | async-done | bytes 6635536 | tf_op jit(solution)/shard_map/all_gather | solution.py:133
  94.0 10.0 %reshape.163 = bf16[1152,2880]{1,0:T(8,128)(2,1)} reshape(bf16[64,18,2880]{2,1,0:T(8,128)(2,1)} %all-gather.4.cloned.1.call-done) | data formatting | bytes 13271040
  104.1 4.3 %fusion.8 = bf16[1,2880,4]{1,2,0:T(4,128)(2,1)S(1)} fusion(bf16[1152,2880]{1,0:T(8,128)(2,1)} %reshape.163, bf16[1152,1152]{1,0:T(8,128)(2,1)S(1)} %copy-done, f32[4,1152]{1,0:T(4,128)S(1)} %fusion.60, bf16[2,1152]{1,0:T(2,128)(2,1)S(1)} %copy-done.9), kind=kOutput, calls=%fused_computation.19 | convolution fusion | flops 37239552 | bytes 9335808 | tf_op jit(solution)/shard_map/dot_general | solution.py:131
  108.4 2.3 %all-gather.1 = bf16[2,2880,4]{1,2,0:T(4,128)(2,1)S(1)} all-gather(bf16[1,2880,4]{1,2,0:T(4,128)(2,1)S(1)} %fusion.8), channel_id=1, replica_groups=mesh['dp'=64,'tensor'=2] {'tensor'}, dimensions={0}, use_global_device_ids=true | all-gather | bytes 69120 | tf_op jit(solution)/shard_map/all_gather | solution.py:136
  110.7 0.1 reshape.168
  110.9 0.1 reshape.161
  111.0 0.1 slice_bitcast_fusion.12
  111.1 0.1 squeeze.32
  111.3 5.6 %fusion.17 = bf16[2,256,3,576]{1,3,2,0:T(8,128)(2,1)S(1)} fusion(bf16[1,1152,3,576]{1,3,2,0:T(8,128)(2,1)} %param.23, f32[2,256,1152]{2,1,0:T(8,128)} %copy-done.2, f32[2,1152]{1,0:T(2,128)S(1)} %get-tuple-element.21, f32[2,1152]{1,0:T(2,128)S(1)} %get-tuple-element.22, f32[2,256]{1,0:T(2,128)S(1)} %add_rsqrt_fusion.3, ...), kind=kOutput, calls=%fused_computation.37 | convolution fusion | flops 2042265600 | bytes 8132608 | tf_op jit(solution)/shard_map/ltd,dck->ltck/dot_general | solution.py:159
  116.8 0.7 fusion.42
  117.6 3.2 %fusion.79 = (f32[2,8,256]{2,1,0:T(8,128)S(1)}, f32[2,8,256,256]{2,3,1,0:T(8,128)S(1)}) fusion(f32[2,8,256,256]{2,3,1,0:T(8,128)S(1)} %fusion.42), kind=kOutput, calls=%fused_computation.139 | output fusion | flops 4194559 | bytes 8404992 | tf_op jit(solution)/shard_map/sub | solution.py:92
  120.8 0.0 copy-start.11
  120.8 0.5 fusion.26
  121.4 0.8 copy-done.11
  122.2 1.2 convolution_convert_fusion.2
  123.4 0.2 broadcast_in_dim.10
  123.5 5.7 %all_to_all.10 = bf16[2,2,256,1152]{3,2,1,0:T(8,128)(2,1)S(1)} all-to-all(bf16[2,2,256,1152]{3,2,1,0:T(8,128)(2,1)S(1)} %broadcast_in_dim.10), channel_id=1, replica_groups=mesh['dp'=64,'tensor'=2] {'tensor'}, dimensions={0} | all-to-all | bytes 4718592 | tf_op jit(solution)/shard_map/all_to_all | solution.py:22
  129.2 0.4 convert_reduce_fusion.1
  129.6 1.3 copy-done.3
  130.9 0.3 fusion.74
  131.3 0.4 multiply_reduce_fusion.4
  131.6 0.0 copy-start.8
  131.6 0.0 copy-start.10
  131.7 0.3 copy-done.13
  132.0 0.6 fusion.39
  132.6 0.2 reshape.156
  132.8 0.1 fusion.73
  132.9 0.1 convert_element_type.99
  133.0 1.8 %fusion.80 = (f32[2,256]{1,0:T(2,128)S(1)}, f32[2,256,1152]{2,1,0:T(8,128)S(1)}) fusion(f32[256,1152]{1,0:T(8,128)} %copy-done.4, bf16[2,256,16]{2,1,0:T(8,128)(2,1)S(1)} %convert_element_type.99, bf16[16,1152]{1,0:T(8,128)(2,1)S(1)} %copy-done.7), kind=kOutput, calls=%fused_computation.140 | convolution fusion | flops 20053504 | bytes 3594240 | tf_op jit(solution)/shard_map/ltc,cd->ltd/dot_general | solution.py:154
  134.8 0.4 multiply_reduce_fusion.3
  135.2 0.1 squeeze.38
  135.4 4.8 %fusion.20 = bf16[2,256,3,576]{1,3,2,0:T(8,128)(2,1)S(1)} fusion(bf16[1,1152,3,576]{1,3,2,0:T(8,128)(2,1)} %param.23, f32[2,256,1152]{2,1,0:T(8,128)S(1)} %get-tuple-element.43, f32[2,1152]{1,0:T(2,128)S(1)} %get-tuple-element.18, f32[2,1152]{1,0:T(2,128)S(1)} %get-tuple-element.19, f32[2,256]{1,0:T(2,128)S(1)} %add_rsqrt_fusion.1, ...), kind=kOutput, calls=%fused_computation.38 | convolution fusion | flops 2042265600 | bytes 8132608 | tf_op jit(solution)/shard_map/ltd,dck->ltck/dot_general | solution.py:159
  140.2 0.7 fusion.41
  141.0 3.2 %fusion.81 = (f32[2,8,256]{2,1,0:T(8,128)S(1)}, f32[2,8,256,256]{2,3,1,0:T(8,128)S(1)}) fusion(f32[2,8,256,256]{2,3,1,0:T(8,128)S(1)} %fusion.41), kind=kOutput, calls=%fused_computation.141 | output fusion | flops 4194559 | bytes 8404992 | tf_op jit(solution)/shard_map/sub | solution.py:92
  144.2 0.0 copy-start.12
  144.2 0.5 fusion.25
  144.7 0.8 copy-done.12
  145.5 1.2 convolution_convert_fusion.1
  146.7 0.2 broadcast_in_dim.11
  146.9 5.6 %all_to_all.11 = bf16[2,2,256,1152]{3,2,1,0:T(8,128)(2,1)S(1)} all-to-all(bf16[2,2,256,1152]{3,2,1,0:T(8,128)(2,1)S(1)} %broadcast_in_dim.11), channel_id=1, replica_groups=mesh['dp'=64,'tensor'=2] {'tensor'}, dimensions={0} | all-to-all | bytes 4718592 | tf_op jit(solution)/shard_map/all_to_all | solution.py:22
  152.5 0.4 convert_reduce_fusion
  152.9 0.4 fusion.72
  153.3 0.4 multiply_reduce_fusion.2
  153.7 0.6 fusion.40
  154.3 0.2 reshape.159
  154.5 0.3 multiply_reduce_fusion.6
  154.8 0.5 multiply_sqrt_fusion
  155.3 0.7 broadcast_select_fusion
  (40 shorter events, 0.2 us)
Async XLA Ops:
  7.2 96.9 %copy-start = (bf16[1152,1152]{1,0:T(8,128)(2,1)S(1)}, bf16[1152,1152]{1,0:T(8,128)(2,1)}, u32[]{:S(2)}) copy-start(bf16[1152,1152]{1,0:T(8,128)(2,1)} %param.22) | copy-start | bytes 7962628
  7.2 7.9 %copy-start.7 = (bf16[16,1152]{1,0:T(8,128)(2,1)S(1)}, bf16[16,1152]{1,0:T(8,128)(2,1)}, u32[]{:S(2)}) copy-start(bf16[16,1152]{1,0:T(8,128)(2,1)} %param.20) | copy-start | bytes 110596
  7.2 86.8 %all-gather.4.cloned.1.call-start = ((), (), s32[]{:S(2)}) async-start(), calls=%async_computation.2 | async-start | bytes 9185280 | tf_op jit(solution)/shard_map/all_gather | solution.py:133
  14.0 1.0 copy-start.4
  15.1 2.3 %copy-start.14 = (s32[2]{0:T(128)S(1)}, s32[2]{0:T(128)}, u32[]{:S(2)}) copy-start(s32[2]{0:T(128)} %param.19) | copy-start | bytes 28
  15.1 2.5 %copy-start.5 = (bf16[256,1152]{1,0:T(8,128)(2,1)S(1)}, bf16[256,1152]{1,0:T(8,128)(2,1)}, u32[]{:S(2)}) copy-start(bf16[256,1152]{1,0:T(8,128)(2,1)} %param.21) | copy-start | bytes 1769476
  15.6 1.4 copy-start.2
  17.7 86.3 %copy-start.9 = (bf16[2,1152]{1,0:T(2,128)(2,1)S(1)}, bf16[2,1152]{1,0:T(2,128)(2,1)}, u32[]{:S(2)}) copy-start(bf16[2,1152]{1,0:T(2,128)(2,1)} %param.16) | copy-start | bytes 13828
  120.8 1.3 copy-start.11
  129.2 1.7 %copy-start.3 = (f32[2,256,1152]{2,1,0:T(8,128)S(1)}, f32[2,256,1152]{2,1,0:T(8,128)}, u32[]{:S(2)}) copy-start(f32[2,256,1152]{2,1,0:T(8,128)} %copy-done.2) | copy-start | bytes 7077892
  131.2 0.8 copy-start.13
  131.6 1.1 copy-start.6
  131.6 1.1 copy-start.8
  131.6 1.1 copy-start.10
  144.2 1.3 copy-start.12
  153.3 2.7 %copy-start.1 = (bf16[1152,1152]{1,0:T(8,128)(2,1)S(1)}, bf16[1152,1152]{1,0:T(8,128)(2,1)}, u32[]{:S(2)}) copy-start(bf16[1152,1152]{1,0:T(8,128)(2,1)} %param.22) | copy-start | bytes 7962628
Sparse Core Ops, SparseCore 0:
  10.9 83.1 all-gather.3
where the time goes:
time: 164 us; the launch traced here: 163 us
  waiting for transfers between devices  76.3 us (47%)
  matrix products  23.3 us (14%)
  other arithmetic  17.9 us (11%)
  local copies, waits for them, and re-layouts  17.2 us (10%)
  between operations  14.5 us (9%)
  blocking collectives  13.6 us (8%)
    all_gather x1, waiting for transfers between devices, shards(): lax.all_gather(packed, 'dp', axis=0, tiled=True)  76.3 us
    unnamed x34, local copies, waits for them, and re-layouts  15.8 us
    all_to_all x2, blocking collectives, from_everyone(): lax.all_to_all(jnp.broadcast_to(array[None], (peers, *array.shape)), axis...  11.2 us
    dot_general x2, matrix products, evaluate(): jnp.einsum('ltd,dck->ltck', attn_in, qkv_weight[0], preferred_element_typ...  10.4 us
    sub x2, other arithmetic, attend(): attn_probs = jax.nn.softmax(scores, axis=-1).astype(jnp.bfloat16)  6.48 us
    dot_general x1, matrix products, shards(): jnp.dot(cond_act, lax.all_gather(packed, 'dp', axis=0, tiled=True), prefe...  4.3 us
  transfers between devices with their start and end apart: 1, of which 1 were waited for; matrix products, arithmetic and copies ran while one was open for 4% of the time, Pallas kernels for 0%

commit v1 on v0

v1 whole, which is shorter than its diff:
```python
import functools
import math

import jax
import jax.numpy as jnp
from jax import lax
from jax.experimental import pallas as pl
from jax.experimental.pallas import tpu as pltpu
from jax.sharding import PartitionSpec as P

MESH = pl.DeviceIdType.MESH
F32 = jnp.float32
BF16 = jnp.bfloat16

D = 1152
TOK = 256
PATCH_VALS = 16
FREQ = 256
HEADS = 16
HEAD_DIM = 72
LATENT = 4096
GROUPS = 2
HALF = D // GROUPS
LANES = 128
CHUNK_ROWS = LATENT // LANES
PER_ROW = LANES // PATCH_VALS
FEATURE_TILES = D // LANES
ADA_TILES = 27
MOD_TILES = 45
CHIPS = 64

beta_low = 0.1
beta_high = 20.0
tol_abs = 0.0078
tol_rel = 0.05
norm_eps = 1e-06


def beta_at(moments):
    return beta_low + (beta_high - beta_low) * moments


def sigma_at(moments):
    integral = beta_low * moments + 0.5 * (beta_high - beta_low) * moments * moments
    return jnp.sqrt(1.0 - jnp.exp(-integral))


def lanes_of(shape):
    return lax.broadcasted_iota(jnp.int32, shape, len(shape) - 1)


def silu(values):
    return values / (1.0 + jnp.exp(-values))


def normed(values):
    average = jnp.sum(values, axis=-1, keepdims=True) * (1.0 / D)
    centred = values - average
    spread_sq = jnp.sum(centred * centred, axis=-1, keepdims=True) * (1.0 / D)
    return centred * lax.rsqrt(spread_sq + norm_eps)


def dot(a, b):
    return jnp.dot(a, b, preferred_element_type=F32)


def dot_t(a, b):
    return lax.dot_general(a, b, (((1,), (1,)), ((), ())), preferred_element_type=F32)


def peer_of(me, step):
    code = step + step // 42
    far_x, far_y, far_z = (code % 4 + 2) % 4, ((code // 4) % 4 + 2) % 4, (code // 16 + 2) % 4
    x, y, z = (me % 4 + far_x) % 4, ((me // 4) % 4 + far_y) % 4, (me // 16 + far_z) % 4
    return z * 16 + y * 4 + x


def kernel(
    now_ref,
    step_ref,
    accept_ref,
    current_ref,
    noise_ref,
    labels_ref,
    patch_ref,
    proj_ref,
    ada_ref,
    final_ref,
    time_in_ref,
    time_out_ref,
    qkv_ref,
    out_ref,
    state_ref,
    error_ref,
    time_in,
    time_out,
    wqkv,
    wout,
    stage,
    cond_send,
    cond_all,
    tiles_all,
    mod_send,
    mods,
    finals,
    patch8,
    proj8,
    table,
    stream,
    normal,
    qkv,
    mixed,
    rows,
    local_sem,
    tile_sem,
    swap_sem,
    cond_sem,
    weight_sem,
    mod_sem,
    final_sem,
):
    me = lax.axis_index("dp")
    side = lax.axis_index("tensor")
    other = 1 - side

    def at(chip, core):
        return {"dp": chip, "tensor": core}

    def own_row(pair):
        return jnp.where(side == 0, pair[0:1], pair[1:2])

    barrier = pltpu.get_barrier_semaphore()
    pl.semaphore_signal(barrier, inc=1, device_id=at(me, other), device_id_type=MESH)

    @pl.loop(0, CHIPS - 1)
    def _(step):
        pl.semaphore_signal(
            barrier, inc=1, device_id=at(peer_of(me, step), side), device_id_type=MESH
        )

    loads = [
        pltpu.make_async_copy(time_in_ref, time_in, local_sem.at[0]),
        pltpu.make_async_copy(time_out_ref, time_out, local_sem.at[1]),
        pltpu.make_async_copy(qkv_ref, wqkv.at[side], local_sem.at[2]),
        pltpu.make_async_copy(out_ref, wout.at[side], local_sem.at[3]),
    ]
    for copy in loads:
        copy.start()

    def put(tile, values):
        for pair in range(9):
            stage[side, tile, pair] = values[2 * pair : 2 * pair + 2]

    blank = jnp.zeros((18, 64), BF16)

    @pl.when(side == 0)
    def _():
        for tile in range(13):
            put(tile, ada_ref[0, :, tile * LANES : (tile + 1) * LANES])
        put(13, jnp.concatenate([ada_ref[0, :, 13 * LANES : 13 * LANES + 64], blank], axis=1))

    @pl.when(side == 1)
    def _():
        put(0, jnp.concatenate([blank, ada_ref[0, :, 0:64]], axis=1))
        for tile in range(1, 14):
            start = tile * LANES - 64
            put(tile, ada_ref[0, :, start : start + LANES])

    for tile in range(FEATURE_TILES):
        put(14 + tile, final_ref[:, tile * LANES : (tile + 1) * LANES])

    time_now = jnp.full((1, LANES), now_ref[side], F32)
    step_size = jnp.full((1, LANES), step_ref[side], F32)
    later = time_now - step_size
    moments = jnp.concatenate([time_now, later, jnp.zeros((6, LANES), F32)], axis=0)
    index = lanes_of((8, LANES)).astype(F32)
    rates = jnp.exp(-math.log(10000.0) * index / (FREQ // 2))
    angles = 1000.0 * moments * rates
    features = jnp.concatenate([jnp.cos(angles), jnp.sin(angles)], axis=1).astype(BF16)
    loads[0].wait()
    hidden = silu(dot(features, time_in[...])).astype(BF16)
    loads[1].wait()
    both = labels_ref[...].astype(F32)
    label = own_row(both)
    cond = silu(label + dot(hidden, time_out[...])).astype(BF16)
    for tile in range(FEATURE_TILES):
        piece = cond[0:2, tile * LANES : (tile + 1) * LANES]
        cond_send[tile] = piece
        cond_all[tile, me] = piece

    pl.semaphore_wait(barrier, CHIPS)

    tile_swap = pltpu.make_async_remote_copy(
        src_ref=stage.at[side],
        dst_ref=stage.at[side],
        send_sem=tile_sem.at[0],
        recv_sem=tile_sem.at[1],
        device_id=at(me, other),
        device_id_type=MESH,
    )
    tile_swap.start()

    @pl.loop(0, CHIPS - 1)
    def _(step):
        pltpu.make_async_remote_copy(
            src_ref=cond_send,
            dst_ref=cond_all.at[:, me],
            send_sem=cond_sem.at[0],
            recv_sem=cond_sem.at[1],
            device_id=at(peer_of(me, step), side),
            device_id_type=MESH,
        ).start()

    tile_swap.wait()
    for pair in range(9):
        stage[0, 13, pair] = stage[0, 13, pair] + stage[1, 0, pair]

    def send_tile(chip, core, tile):
        @pl.when(chip != me)
        def _():
            pltpu.make_async_remote_copy(
                src_ref=stage.at[core, tile],
                dst_ref=tiles_all.at[pl.ds(me * 9, 9)],
                send_sem=weight_sem.at[0],
                recv_sem=weight_sem.at[1],
                device_id=at(chip, side),
                device_id_type=MESH,
            ).start()

        @pl.when(chip == me)
        def _():
            tiles_all[pl.ds(me * 9, 9)] = stage[core, tile]

    @pl.loop(0, 14)
    def _(i):
        send_tile(i, 0, i)

    @pl.loop(14, 27)
    def _(i):
        send_tile(i, 1, i - 13)

    @pl.loop(27, 36)
    def _(i):
        send_tile(i, 0, i - 13)

    @pl.loop(36, 45)
    def _(i):
        send_tile(i, 1, i - 22)

    swaps = []
    for slot, (src, dst) in enumerate(((qkv_ref, wqkv), (out_ref, wout))):
        swaps.append(
            pltpu.make_async_remote_copy(
                src_ref=src,
                dst_ref=dst.at[side],
                send_sem=swap_sem.at[slot],
                recv_sem=swap_sem.at[2 + slot],
                device_id=at(me, other),
                device_id_type=MESH,
            )
        )
        swaps[-1].start()

    lane8 = lanes_of((CHUNK_ROWS, LANES)) // PATCH_VALS
    for piece in range(CHUNK_ROWS):
        span = slice(piece * LANES, (piece + 1) * LANES)
        rows[0, piece : piece + 1, :] = own_row(current_ref[:, span])
        rows[1, piece : piece + 1, :] = own_row(noise_ref[:, span])
    current = rows[0]
    draw = rows[1]
    for copy in range(PER_ROW):
        patch8[copy * PATCH_VALS : (copy + 1) * PATCH_VALS, :] = patch_ref[...]
    spread_lanes = (
        lax.broadcasted_iota(jnp.int32, (LANES, PATCH_VALS), 0) % PATCH_VALS
        == lanes_of((LANES, PATCH_VALS))
    )
    proj8[...] = dot(jnp.where(spread_lanes, 1.0, 0.0).astype(BF16), proj_ref[...]).astype(BF16)

    half = D // 2
    fill = jnp.zeros((TOK, 64), BF16)
    for group in range(GROUPS):
        for part in range(3):
            qkv[group, part, :, HALF:] = fill

    def table_chunk(j, carry):
        place = lax.broadcasted_iota(jnp.int32, (CHUNK_ROWS, D), 0) * PER_ROW + j
        column = lanes_of((CHUNK_ROWS, D))
        first = column < half
        freq = jnp.where(first, column, column - half).astype(F32)
        angle = place.astype(F32) * jnp.exp(-math.log(10000.0) * freq / half)
        table[pl.ds(pl.multiple_of(j * CHUNK_ROWS, CHUNK_ROWS), CHUNK_ROWS), :] = jnp.where(
            first, jnp.sin(angle), jnp.cos(angle)
        )
        return carry

    lax.fori_loop(0, PER_ROW, table_chunk, 0)

    def drain(ref, sem):
        pltpu.make_async_copy(ref, ref, sem).wait()

    drain(cond_all.at[:, pl.ds(0, CHIPS - 1)], cond_sem.at[1])

    @pl.when(me < MOD_TILES)
    def _():
        drain(tiles_all.at[pl.ds(0, 9 * (CHIPS - 1))], weight_sem.at[1])
        total = jnp.zeros((2 * CHIPS, LANES), F32)
        for tile in range(FEATURE_TILES):
            lhs = cond_all[tile].reshape(2 * CHIPS, LANES)
            rhs = tiles_all[tile * 64 : (tile + 1) * 64].reshape(LANES, LANES)
            total = total + dot(lhs, rhs)
        mod_send[...] = total.reshape(CHIPS, 2, LANES)
        mods[me] = mod_send[me]

        @pl.loop(0, CHIPS - 1)
        def _(step):
            chip = peer_of(me, step)
            pltpu.make_async_remote_copy(
                src_ref=mod_send.at[chip],
                dst_ref=mods.at[me],
                send_sem=mod_sem.at[0],
                recv_sem=mod_sem.at[1],
                device_id=at(chip, side),
                device_id_type=MESH,
            ).start()

    @pl.when(me < MOD_TILES)
    def _():
        drain(mods.at[pl.ds(0, MOD_TILES - 1)], mod_sem.at[1])

    @pl.when(me >= MOD_TILES)
    def _():
        drain(mods, mod_sem.at[1])

    loads[2].wait()
    loads[3].wait()
    for swap in swaps:
        swap.wait()

    def mod_row(which, moment):
        tiles = [mods[which * FEATURE_TILES + tile] for tile in range(FEATURE_TILES)]
        pair = jnp.concatenate(tiles, axis=1)
        return jnp.where(moment == 0, pair[0:1], pair[1:2])

    exponent = HEAD_DIM ** (-0.5) * math.log2(math.e)

    def evaluate(latent, moment):
        tokens = jnp.concatenate(
            [jnp.where(lane8 == j, latent, 0.0) for j in range(PER_ROW)], axis=0
        ).astype(BF16)
        stream[...] = dot(tokens, patch8[...]) + table[...]
        shift, scale = mod_row(0, moment), 1.0 + mod_row(1, moment)
        for j in range(PER_ROW):
            span = slice(j * CHUNK_ROWS, (j + 1) * CHUNK_ROWS)
            normal[span] = (normed(stream[span]) * scale + shift).astype(BF16)

        for group in range(GROUPS):
            for part in range(3):
                qkv[group, part, :, :HALF] = dot_t(normal[...], wqkv[group, part]).astype(BF16)

        def attend(group, carry):
            for head in range(HEADS // GROUPS):
                low, high = head * HEAD_DIM, (head + 1) * HEAD_DIM
                left = low // LANES * LANES
                right = -(-high // LANES) * LANES
                lane = lanes_of((1, right - left)) + left
                own = (lane >= low) & (lane < high)
                queries = qkv[group, 0, :, left:right]
                queries = jnp.where(own, queries, jnp.zeros_like(queries))
                scores = dot_t(queries, qkv[group, 1, :, left:right])
                top = jnp.max(scores, axis=-1, keepdims=True)
                weights = jnp.exp2((scores - top) * exponent)
                whole = jnp.sum(weights, axis=-1, keepdims=True)
                probs = (weights * (1.0 / whole)).astype(BF16)
                result = dot(probs, qkv[group, 2, :, left:right])
                for start in range(left, right, LANES):
                    piece = result[:, start - left : start - left + LANES]
                    if low > start:
                        past = lanes_of((1, LANES)) + start >= low
                        piece = jnp.where(past, piece, mixed[group, :, start : start + LANES].astype(F32))
                    mixed[group, :, start : start + LANES] = piece.astype(BF16)
            return carry

        lax.fori_loop(0, GROUPS, attend, 0)

        partial = [
            dot(mixed[group, :, :HALF], wout[group]).astype(BF16).astype(F32)
            for group in range(GROUPS)
        ]
        stream[...] = stream[...] + mod_row(2, moment) * (partial[0] + partial[1])
        shift, scale = mod_row(3, moment), 1.0 + mod_row(4, moment)
        for j in range(PER_ROW):
            span = slice(j * CHUNK_ROWS, (j + 1) * CHUNK_ROWS)
            normal[span] = (normed(stream[span]) * scale + shift).astype(BF16)
        guessed = dot_t(normal[...], proj8[...])
        result = jnp.zeros((CHUNK_ROWS, LANES), F32)
        for j in range(PER_ROW):
            result = result + jnp.where(
                lane8 == j, guessed[j * CHUNK_ROWS : (j + 1) * CHUNK_ROWS], 0.0
            )
        return result

    spread = jnp.sqrt(step_size * beta_at(time_now)) * draw

    rows[2] = current

    def one_moment(moment, carry):
        guess = evaluate(rows[2], moment)
        rows[4] = guess

        @pl.when(moment == 0)
        def _():
            rows[3] = guess
            beta = beta_at(time_now)
            drift_now = 0.5 * beta * rows[0] - beta * guess / sigma_at(time_now)
            rows[2] = rows[0] + step_size * drift_now + spread

        return carry

    lax.fori_loop(0, 2, one_moment, 0)

    current = rows[0]
    beta = beta_at(time_now)
    drift_now = 0.5 * beta * current - beta * rows[3] / sigma_at(time_now)
    euler = rows[2]
    beta_then = beta_at(later)
    drift_later = 0.5 * beta_then * euler - beta_then * rows[4] / sigma_at(later)
    heun = current + 0.5 * step_size * (drift_now + drift_later) + spread
    scale_ref = jnp.maximum(tol_abs, tol_rel * jnp.maximum(jnp.abs(heun), jnp.abs(current)))
    gap = (euler - heun) / scale_ref
    squares = jnp.sum(jnp.sum(gap * gap, axis=1, keepdims=True), axis=0, keepdims=True)
    error = jnp.sqrt(squares / LATENT)
    taken = jnp.full((CHUNK_ROWS, LANES), accept_ref[side], jnp.int32) == 1
    finals[side, :CHUNK_ROWS] = jnp.where(taken, heun, current)
    finals[side, CHUNK_ROWS:] = jnp.broadcast_to(error, (8, LANES))
    final_swap = pltpu.make_async_remote_copy(
        src_ref=finals.at[side],
        dst_ref=finals.at[side],
        send_sem=final_sem.at[0],
        recv_sem=final_sem.at[1],
        device_id=at(me, other),
        device_id_type=MESH,
    )
    final_swap.start()

    drain(cond_all.at[:, pl.ds(0, CHIPS - 1)], cond_sem.at[0])
    @pl.when(me >= MOD_TILES)
    def _():
        drain(tiles_all.at[pl.ds(0, 9 * MOD_TILES)], weight_sem.at[0])

    @pl.when(me < MOD_TILES)
    def _():
        drain(tiles_all.at[pl.ds(0, 9 * (MOD_TILES - 1))], weight_sem.at[0])
        drain(mod_send.at[pl.ds(0, CHIPS - 1)], mod_sem.at[0])

    final_swap.wait()
    for latent in range(2):
        for piece in range(CHUNK_ROWS):
            state_ref[latent : latent + 1, piece * LANES : (piece + 1) * LANES] = finals[
                latent, piece : piece + 1, :
            ]
        error_ref[latent : latent + 1, :] = finals[latent, CHUNK_ROWS : CHUNK_ROWS + 1, :]


def shards(
    current,
    noise_draw,
    labels,
    time_now,
    step_size,
    accept,
    patch_weight,
    time_in,
    time_out,
    qkv_weight,
    out_weight,
    ada_weight,
    final_ada,
    final_proj,
):
    smem = pl.BlockSpec(memory_space=pltpu.SMEM)
    vmem = pl.BlockSpec(memory_space=pltpu.VMEM)
    place = pl.BlockSpec(memory_space=pl.ANY)
    state, error = pl.pallas_call(
        kernel,
        out_shape=(
            jax.ShapeDtypeStruct((2, LATENT), F32),
            jax.ShapeDtypeStruct((2, LANES), F32),
        ),
        in_specs=[smem] * 3 + [vmem] * 7 + [place] * 4,
        out_specs=(vmem, vmem),
        scratch_shapes=[
            pltpu.VMEM((FREQ, D), BF16),
            pltpu.VMEM((D, D), BF16),
            pltpu.VMEM((GROUPS, 3, HALF, D), BF16),
            pltpu.VMEM((GROUPS, HALF, D), BF16),
            pltpu.VMEM((2, 23, 9, 2, LANES), BF16),
            pltpu.VMEM((FEATURE_TILES, 2, LANES), BF16),
            pltpu.VMEM((FEATURE_TILES, CHIPS, 2, LANES), BF16),
            pltpu.VMEM((9 * CHIPS, 2, LANES), BF16),
            pltpu.VMEM((CHIPS, 2, LANES), F32),
            pltpu.VMEM((MOD_TILES, 2, LANES), F32),
            pltpu.VMEM((2, CHUNK_ROWS + 8, LANES), F32),
            pltpu.VMEM((LANES, D), BF16),
            pltpu.VMEM((LANES, D), BF16),
            pltpu.VMEM((TOK, D), F32),
            pltpu.VMEM((TOK, D), F32),
            pltpu.VMEM((TOK, D), BF16),
            pltpu.VMEM((GROUPS, 3, TOK, 640), BF16),
            pltpu.VMEM((GROUPS, TOK, 640), BF16),
            pltpu.VMEM((5, CHUNK_ROWS, LANES), F32),
            pltpu.SemaphoreType.DMA((4,)),
            pltpu.SemaphoreType.DMA((2,)),
            pltpu.SemaphoreType.DMA((4,)),
            pltpu.SemaphoreType.DMA((2,)),
            pltpu.SemaphoreType.DMA((2,)),
            pltpu.SemaphoreType.DMA((2,)),
            pltpu.SemaphoreType.DMA((2,)),
        ],
        compiler_params=pltpu.CompilerParams(
            collective_id=0, has_side_effects=True, vmem_limit_bytes=60 * 1024 * 1024
        ),
        name="heun_step",
    )(
        time_now,
        step_size,
        accept,
        current,
        noise_draw,
        labels,
        patch_weight,
        final_proj.T,
        ada_weight,
        final_ada,
        time_in,
        time_out,
        qkv_weight[0].transpose(1, 2, 0),
        out_weight[0].T,
    )
    return state, error[:, 0]


def solution(mesh):
    in_specs = (
        P("dp", None),
        P("dp", None),
        P("dp", None),
        P("dp"),
        P("dp"),
        P("dp"),
        P(),
        P(),
        P(),
        P(None, None, None, "tensor"),
        P(None, None, "tensor"),
        P(None, "dp", "tensor"),
        P("dp", "tensor"),
        P(),
    )
    out_specs = (P("dp", None), P("dp"))
    return jax.shard_map(shards, mesh=mesh, in_specs=in_specs, out_specs=out_specs, check_vma=False)
```

time: 164 us -> 53.9 us (0.33)
  waiting for transfers between devices: 76.3 us -> 0 us
  Pallas kernels: 0 us -> 50.3 us
  matrix products: 23.3 us -> 0 us
  other arithmetic: 17.9 us -> 0 us
  local copies, waits for them, and re-layouts: 17.2 us -> 2.65 us
  between operations: 14.5 us -> 0.64 us
  blocking collectives: 13.6 us -> 0 us
    all_gather x1 -> x0, waiting for transfers between devices: 76.3 us -> none  [shards(): lax.all_gather(packed, 'dp', axis=0, tiled=True)]
    pallas_call x0 -> x1, Pallas kernels: none -> 50.3 us  [shards(): pl.pallas_call(kernel, out_shape=(jax.ShapeDtypeStruct((2, LATENT), F32),...]
    dot_general x14 -> x0, matrix products: 23.3 us -> none  [the longest x2 10.4 us: evaluate(): jnp.einsum('ltd,dck->ltck', attn_in, qkv_weight[0], preferred_element_typ...]
    unnamed x34 -> x1, local copies, waits for them, and re-layouts: 15.8 us -> 1.37 us
    all_to_all x2 -> x0, blocking collectives: 11.2 us -> none  [from_everyone(): lax.all_to_all(jnp.broadcast_to(array[None], (peers, *array.shape)), axis...]
    sub x2 -> x0, other arithmetic: 6.48 us -> none  [attend(): attn_probs = jax.nn.softmax(scores, axis=-1).astype(jnp.bfloat16)]
    reduce_sum x9 -> x0, other arithmetic: 3.26 us -> none  [the longest x4 1.49 us: layer_norm(): spread_sq = jnp.mean(centred * centred, axis=-1, keepdims=True)]
    sin x1 -> x0, other arithmetic: 2.35 us -> none  [position_table(): return jnp.concatenate([jnp.sin(angles), jnp.cos(angles)], axis=1)]
  transfers between devices with their start and end apart: 1 -> 0, of which waited for: 1 -> 0; matrix products, arithmetic and copies ran while one was open for 4% -> 0% of each run, Pallas kernels for 0% -> 0%
where the time goes in v1:
time: 53.9 us; the launch traced here: 53.6 us
  Pallas kernels  50.3 us (93%)
  local copies, waits for them, and re-layouts  2.65 us (5%)
  between operations  0.64 us (1%)
    pallas_call x1, Pallas kernels, shards(): pl.pallas_call(kernel, out_shape=(jax.ShapeDtypeStruct((2, LATENT), F32),...  50.3 us
    unnamed x1, local copies, waits for them, and re-layouts  1.37 us
    slice x1, local copies, waits for them, and re-layouts, shards(): return (state, error[:, 0])  1.28 us

profile of v1, /device:TPU:1, one launch (start us, length us, event | category | flops | bytes accessed | tf_op | source)
XLA Modules:
  0.0 53.6 jit_solution(14602766268372130430)
XLA Ops:
  0.6 50.3 %heun_step.1 = (f32[2,4096]{1,0:T(2,128)}, f32[2,128]{1,0:T(2,128)}) custom-call(f32[2]{0:T(128)} %now_ref.1, f32[2]{0:T(128)} %step_ref.1, s32[2]{0:T(128)} %accept_ref.1, f32[2,4096]{1,0:T(2,128)} %current_ref.1, f32[2,4096]{1,0:T(2,128)} %noise_ref.1, bf16[2,1152]{1,0:T(2,128)(2,1)} %labels_ref.1, bf16[16,1152]{1,0:T(8,128)(2,1)} %patch_ref.1, ...), custom_call_target="tpu_custom_call" | custom-call | tf_op jit(solution)/shard_map/heun_step/pallas_call | solution.py:483
  51.0 1.3 %slice_reduce_fusion = f32[2]{0:T(128)} fusion(f32[2,128]{1,0:T(2,128)} %get-tuple-element.5), kind=kLoop, calls=%fused_computation | loop fusion | bytes 16 | tf_op jit(solution)/shard_map/slice | solution.py:539
  52.3 1.4 %copy.17 = f32[2,4096]{1,0:T(2,128)} copy(f32[2,4096]{1,0:T(2,128)} %get-tuple-element.8) | data formatting | bytes 65536

commit v2 on v1

--- a/solution.py
+++ b/solution.py
@@ -25,9 +25,15 @@
 CHUNK_ROWS = LATENT // LANES
 PER_ROW = LANES // PATCH_VALS
 FEATURE_TILES = D // LANES
-ADA_TILES = 27
 MOD_TILES = 45
 CHIPS = 64
+TILE_CHIPS = (
+    tuple(range(9)),
+    (9, 10, 11, 12, 13, 23, 24, 25, 26),
+    tuple(range(27, 36)),
+    tuple(range(14, 23)),
+    tuple(range(36, 45)),
+)
 
 beta_low = 0.1
 beta_high = 20.0
@@ -68,11 +74,10 @@
     return lax.dot_general(a, b, (((1,), (1,)), ((), ())), preferred_element_type=F32)
 
 
-def peer_of(me, step):
-    code = step + step // 42
-    far_x, far_y, far_z = (code % 4 + 2) % 4, ((code // 4) % 4 + 2) % 4, (code // 16 + 2) % 4
-    x, y, z = (me % 4 + far_x) % 4, ((me // 4) % 4 + far_y) % 4, (me // 16 + far_z) % 4
-    return z * 16 + y * 4 + x
+OFFSETS = sorted(
+    ((z, y, x) for z in (2, 1, 3, 0) for y in (2, 1, 3, 0) for x in (2, 1, 3, 0) if z + y + x),
+    key=lambda offset: -sum(min(step, 4 - step) for step in offset),
+)
 
 
 def kernel(
@@ -108,8 +113,13 @@
     table,
     stream,
     normal,
-    qkv,
+    queries,
+    keys,
+    values,
     mixed,
+    turned,
+    scores,
+    probs,
     rows,
     local_sem,
     tile_sem,
@@ -132,16 +142,17 @@
     barrier = pltpu.get_barrier_semaphore()
     pl.semaphore_signal(barrier, inc=1, device_id=at(me, other), device_id_type=MESH)
 
-    @pl.loop(0, CHIPS - 1)
-    def _(step):
-        pl.semaphore_signal(
-            barrier, inc=1, device_id=at(peer_of(me, step), side), device_id_type=MESH
-        )
+    along_x = [lax.rem(me + step, 4) for step in range(4)]
+    along_y = [lax.rem(me // 4 + step, 4) * 4 for step in range(4)]
+    along_z = [lax.rem(me // 16 + step, 4) * 16 for step in range(4)]
+    peers = [along_z[z] + along_y[y] + along_x[x] for z, y, x in OFFSETS]
+    for chip in peers:
+        pl.semaphore_signal(barrier, inc=1, device_id=at(chip, side), device_id_type=MESH)
 
     loads = [
         pltpu.make_async_copy(time_in_ref, time_in, local_sem.at[0]),
         pltpu.make_async_copy(time_out_ref, time_out, local_sem.at[1]),
-        pltpu.make_async_copy(qkv_ref, wqkv.at[side], local_sem.at[2]),
+        pltpu.make_async_copy(qkv_ref, wqkv.at[:, side], local_sem.at[2]),
         pltpu.make_async_copy(out_ref, wout.at[side], local_sem.at[3]),
     ]
     for copy in loads:
@@ -149,7 +160,7 @@
 
     def put(tile, values):
         for pair in range(9):
-            stage[side, tile, pair] = values[2 * pair : 2 * pair + 2]
+            stage[tile, pair] = values[2 * pair : 2 * pair + 2]
 
     blank = jnp.zeros((18, 64), BF16)
 
@@ -157,17 +168,18 @@
     def _():
         for tile in range(13):
             put(tile, ada_ref[0, :, tile * LANES : (tile + 1) * LANES])
+        for tile in range(FEATURE_TILES):
+            put(14 + tile, final_ref[:, tile * LANES : (tile + 1) * LANES])
         put(13, jnp.concatenate([ada_ref[0, :, 13 * LANES : 13 * LANES + 64], blank], axis=1))
 
     @pl.when(side == 1)
     def _():
-        put(0, jnp.concatenate([blank, ada_ref[0, :, 0:64]], axis=1))
+        put(MOD_TILES, jnp.concatenate([blank, ada_ref[0, :, 0:64]], axis=1))
         for tile in range(1, 14):
             start = tile * LANES - 64
-            put(tile, ada_ref[0, :, start : start + LANES])
-
-    for tile in range(FEATURE_TILES):
-        put(14 + tile, final_ref[:, tile * LANES : (tile + 1) * LANES])
+            put(22 + tile, ada_ref[0, :, start : start + LANES])
+        for tile in range(FEATURE_TILES):
+            put(36 + tile, final_ref[:, tile * LANES : (tile + 1) * LANES])
 
     time_now = jnp.full((1, LANES), now_ref[side], F32)
     step_size = jnp.full((1, LANES), step_ref[side], F32)
@@ -191,8 +203,8 @@
     pl.semaphore_wait(barrier, CHIPS)
 
     tile_swap = pltpu.make_async_remote_copy(
-        src_ref=stage.at[side],
-        dst_ref=stage.at[side],
+        src_ref=stage.at[pl.ds(side * 23, 23)],
+        dst_ref=stage.at[pl.ds(side * 23, 23)],
         send_sem=tile_sem.at[0],
         recv_sem=tile_sem.at[1],
         device_id=at(me, other),
@@ -200,26 +212,26 @@
     )
     tile_swap.start()
 
-    @pl.loop(0, CHIPS - 1)
-    def _(step):
+    for chip in peers:
         pltpu.make_async_remote_copy(
             src_ref=cond_send,
             dst_ref=cond_all.at[:, me],
             send_sem=cond_sem.at[0],
             recv_sem=cond_sem.at[1],
-            device_id=at(peer_of(me, step), side),
+            device_id=at(chip, side),
             device_id_type=MESH,
         ).start()
 
     tile_swap.wait()
     for pair in range(9):
-        stage[0, 13, pair] = stage[0, 13, pair] + stage[1, 0, pair]
-
-    def send_tile(chip, core, tile):
-        @pl.when(chip != me)
+        stage[13, pair] = stage[13, pair] + stage[MOD_TILES, pair]
+
+    for chip in peers:
+
+        @pl.when(chip < MOD_TILES)
         def _():
             pltpu.make_async_remote_copy(
-                src_ref=stage.at[core, tile],
+                src_ref=stage.at[chip],
                 dst_ref=tiles_all.at[pl.ds(me * 9, 9)],
                 send_sem=weight_sem.at[0],
                 recv_sem=weight_sem.at[1],
@@ -227,32 +239,16 @@
                 device_id_type=MESH,
             ).start()
 
-        @pl.when(chip == me)
-        def _():
-            tiles_all[pl.ds(me * 9, 9)] = stage[core, tile]
-
-    @pl.loop(0, 14)
-    def _(i):
-        send_tile(i, 0, i)
-
-    @pl.loop(14, 27)
-    def _(i):
-        send_tile(i, 1, i - 13)
-
-    @pl.loop(27, 36)
-    def _(i):
-        send_tile(i, 0, i - 13)
-
-    @pl.loop(36, 45)
-    def _(i):
-        send_tile(i, 1, i - 22)
+    @pl.when(me < MOD_TILES)
+    def _():
+        tiles_all[pl.ds(me * 9, 9)] = stage[me]
 
     swaps = []
-    for slot, (src, dst) in enumerate(((qkv_ref, wqkv), (out_ref, wout))):
+    for slot, (src, dst) in enumerate(((qkv_ref, wqkv.at[:, side]), (out_ref, wout.at[side]))):
         swaps.append(
             pltpu.make_async_remote_copy(
                 src_ref=src,
-                dst_ref=dst.at[side],
+                dst_ref=dst,
                 send_sem=swap_sem.at[slot],
                 recv_sem=swap_sem.at[2 + slot],
                 device_id=at(me, other),
@@ -277,11 +273,6 @@
     proj8[...] = dot(jnp.where(spread_lanes, 1.0, 0.0).astype(BF16), proj_ref[...]).astype(BF16)
 
     half = D // 2
-    fill = jnp.zeros((TOK, 64), BF16)
-    for group in range(GROUPS):
-        for part in range(3):
-            qkv[group, part, :, HALF:] = fill
-
     def table_chunk(j, carry):
         place = lax.broadcasted_iota(jnp.int32, (CHUNK_ROWS, D), 0) * PER_ROW + j
         column = lanes_of((CHUNK_ROWS, D))
@@ -311,9 +302,7 @@
         mod_send[...] = total.reshape(CHIPS, 2, LANES)
         mods[me] = mod_send[me]
 
-        @pl.loop(0, CHIPS - 1)
-        def _(step):
-            chip = peer_of(me, step)
+        for chip in peers:
             pltpu.make_async_remote_copy(
                 src_ref=mod_send.at[chip],
                 dst_ref=mods.at[me],
@@ -337,7 +326,7 @@
         swap.wait()
 
     def mod_row(which, moment):
-        tiles = [mods[which * FEATURE_TILES + tile] for tile in range(FEATURE_TILES)]
+        tiles = [mods[chip] for chip in TILE_CHIPS[which]]
         pair = jnp.concatenate(tiles, axis=1)
         return jnp.where(moment == 0, pair[0:1], pair[1:2])
 
@@ -353,40 +342,51 @@
             span = slice(j * CHUNK_ROWS, (j + 1) * CHUNK_ROWS)
             normal[span] = (normed(stream[span]) * scale + shift).astype(BF16)
 
-        for group in range(GROUPS):
-            for part in range(3):
-                qkv[group, part, :, :HALF] = dot_t(normal[...], wqkv[group, part]).astype(BF16)
-
-        def attend(group, carry):
-            for head in range(HEADS // GROUPS):
-                low, high = head * HEAD_DIM, (head + 1) * HEAD_DIM
-                left = low // LANES * LANES
-                right = -(-high // LANES) * LANES
-                lane = lanes_of((1, right - left)) + left
-                own = (lane >= low) & (lane < high)
-                queries = qkv[group, 0, :, left:right]
-                queries = jnp.where(own, queries, jnp.zeros_like(queries))
-                scores = dot_t(queries, qkv[group, 1, :, left:right])
-                top = jnp.max(scores, axis=-1, keepdims=True)
-                weights = jnp.exp2((scores - top) * exponent)
-                whole = jnp.sum(weights, axis=-1, keepdims=True)
-                probs = (weights * (1.0 / whole)).astype(BF16)
-                result = dot(probs, qkv[group, 2, :, left:right])
-                for start in range(left, right, LANES):
-                    piece = result[:, start - left : start - left + LANES]
-                    if low > start:
-                        past = lanes_of((1, LANES)) + start >= low
-                        piece = jnp.where(past, piece, mixed[group, :, start : start + LANES].astype(F32))
-                    mixed[group, :, start : start + LANES] = piece.astype(BF16)
-            return carry
-
-        lax.fori_loop(0, GROUPS, attend, 0)
-
-        partial = [
-            dot(mixed[group, :, :HALF], wout[group]).astype(BF16).astype(F32)
-            for group in range(GROUPS)
-        ]
-        stream[...] = stream[...] + mod_row(2, moment) * (partial[0] + partial[1])
+        turned[...] = normal[...].T
+        weight = [wqkv[part].reshape(D, D) for part in range(3)]
+        queries[...] = (dot(weight[0], turned[...]) * exponent).astype(BF16)
+        keys[...] = dot(weight[1], turned[...]).astype(BF16).T
+        values[...] = dot(weight[2], turned[...]).astype(BF16)
+
+        def score(head):
+            low, high = head * HEAD_DIM, (head + 1) * HEAD_DIM
+            left = low // LANES * LANES
+            right = -(-high // LANES) * LANES
+            row = lax.broadcasted_iota(jnp.int32, (right - left, 1), 0) + left
+            asked = queries[left:right]
+            asked = jnp.where((row >= low) & (row < high), asked, jnp.zeros_like(asked))
+            scores[head % 2] = dot(keys[:, left:right], asked)
+
+        def soften(head):
+            found = scores[head % 2]
+            weights = jnp.exp2(found - jnp.max(found, axis=0, keepdims=True))
+            probs[head % 2] = weights.astype(BF16)
+            return jnp.sum(weights, axis=0, keepdims=True)
+
+        def apply(head, whole):
+            low, high = head * HEAD_DIM, (head + 1) * HEAD_DIM
+            first = low // 16 * 16
+            result = dot(values[first : first + 80], probs[head % 2])
+            mixed[low:high] = result[low - first : high - first] * (1.0 / whole)
+
+        score(0)
+        before = None
+        for head in range(HEADS):
+            if head + 1 < HEADS:
+                score(head + 1)
+            whole = soften(head)
+            if head:
+                apply(head - 1, before)
+            before = whole
+        apply(HEADS - 1, before)
+
+        attended = lax.dot_general(
+            mixed[...].astype(BF16),
+            wout[...].reshape(D, D),
+            (((0,), (0,)), ((), ())),
+            preferred_element_type=F32,
+        )
+        stream[...] = stream[...] + mod_row(2, moment) * attended
         shift, scale = mod_row(3, moment), 1.0 + mod_row(4, moment)
         for j in range(PER_ROW):
             span = slice(j * CHUNK_ROWS, (j + 1) * CHUNK_ROWS)
@@ -491,9 +491,9 @@
         scratch_shapes=[
             pltpu.VMEM((FREQ, D), BF16),
             pltpu.VMEM((D, D), BF16),
-            pltpu.VMEM((GROUPS, 3, HALF, D), BF16),
+            pltpu.VMEM((3, GROUPS, HALF, D), BF16),
             pltpu.VMEM((GROUPS, HALF, D), BF16),
-            pltpu.VMEM((2, 23, 9, 2, LANES), BF16),
+            pltpu.VMEM((MOD_TILES + 1, 9, 2, LANES), BF16),
             pltpu.VMEM((FEATURE_TILES, 2, LANES), BF16),
             pltpu.VMEM((FEATURE_TILES, CHIPS, 2, LANES), BF16),
             pltpu.VMEM((9 * CHIPS, 2, LANES), BF16),
@@ -505,8 +505,13 @@
             pltpu.VMEM((TOK, D), F32),
             pltpu.VMEM((TOK, D), F32),
             pltpu.VMEM((TOK, D), BF16),
-            pltpu.VMEM((GROUPS, 3, TOK, 640), BF16),
-            pltpu.VMEM((GROUPS, TOK, 640), BF16),
+            pltpu.VMEM((D, TOK), BF16),
+            pltpu.VMEM((TOK, D), BF16),
+            pltpu.VMEM((D, TOK), BF16),
+            pltpu.VMEM((D, TOK), F32),
+            pltpu.VMEM((D, TOK), BF16),
+            pltpu.VMEM((2, TOK, TOK), F32),
+            pltpu.VMEM((2, TOK, TOK), BF16),
             pltpu.VMEM((5, CHUNK_ROWS, LANES), F32),
             pltpu.SemaphoreType.DMA((4,)),
             pltpu.SemaphoreType.DMA((2,)),

time: 53.9 us -> 45 us (0.83)
  Pallas kernels: 50.3 us -> 41.5 us
    pallas_call x1, Pallas kernels: 50.3 us -> 41.5 us  [shards(): pl.pallas_call(kernel, out_shape=(jax.ShapeDtypeStruct((2, LATENT), F32),...]
where the time goes in v2:
time: 45 us; the launch traced here: 44.8 us
  Pallas kernels  41.5 us (92%)
  local copies, waits for them, and re-layouts  2.65 us (6%)
  between operations  0.64 us (1%)
    pallas_call x1, Pallas kernels, shards(): pl.pallas_call(kernel, out_shape=(jax.ShapeDtypeStruct((2, LATENT), F32),...  41.5 us
    unnamed x1, local copies, waits for them, and re-layouts  1.37 us
    slice x1, local copies, waits for them, and re-layouts, shards(): return (state, error[:, 0])  1.28 us

profile of v2, /device:TPU:1, one launch (start us, length us, event | category | flops | bytes accessed | tf_op | source)
XLA Modules:
  0.0 44.8 jit_solution(15741675668997329410)
XLA Ops:
  0.6 41.5 %heun_step.1 = (f32[2,4096]{1,0:T(2,128)}, f32[2,128]{1,0:T(2,128)}) custom-call(f32[2]{0:T(128)} %now_ref.1, f32[2]{0:T(128)} %step_ref.1, s32[2]{0:T(128)} %accept_ref.1, f32[2,4096]{1,0:T(2,128)} %current_ref.1, f32[2,4096]{1,0:T(2,128)} %noise_ref.1, bf16[2,1152]{1,0:T(2,128)(2,1)} %labels_ref.1, bf16[16,1152]{1,0:T(8,128)(2,1)} %patch_ref.1, ...), custom_call_target="tpu_custom_call" | custom-call | tf_op jit(solution)/shard_map/heun_step/pallas_call | solution.py:483
  42.2 1.3 %slice_reduce_fusion = f32[2]{0:T(128)} fusion(f32[2,128]{1,0:T(2,128)} %get-tuple-element.5), kind=kLoop, calls=%fused_computation | loop fusion | bytes 16 | tf_op jit(solution)/shard_map/slice | solution.py:544
  43.4 1.4 %copy.17 = f32[2,4096]{1,0:T(2,128)} copy(f32[2,4096]{1,0:T(2,128)} %get-tuple-element.8) | data formatting | bytes 65536

commit v3 on v2

--- a/solution.py
+++ b/solution.py
@@ -25,7 +25,8 @@
 CHUNK_ROWS = LATENT // LANES
 PER_ROW = LANES // PATCH_VALS
 FEATURE_TILES = D // LANES
-MOD_TILES = 45
+MOD_TILES = 46
+SIDE_TILES = 23
 CHIPS = 64
 TILE_CHIPS = (
     tuple(range(9)),
@@ -59,11 +60,14 @@
     return values / (1.0 + jnp.exp(-values))
 
 
-def normed(values):
-    average = jnp.sum(values, axis=-1, keepdims=True) * (1.0 / D)
-    centred = values - average
-    spread_sq = jnp.sum(centred * centred, axis=-1, keepdims=True) * (1.0 / D)
-    return centred * lax.rsqrt(spread_sq + norm_eps)
+def moments_of(ref, spans):
+    means = [jnp.sum(ref[span], axis=-1, keepdims=True) * (1.0 / D) for span in spans]
+    spreads = []
+    for span, mean in zip(spans, means):
+        centred = ref[span] - mean
+        spread_sq = jnp.sum(centred * centred, axis=-1, keepdims=True) * (1.0 / D)
+        spreads.append(lax.rsqrt(spread_sq + norm_eps))
+    return means, spreads
 
 
 def dot(a, b):
@@ -81,6 +85,22 @@
 
 
 def kernel(
+    now_in,
+    step_in,
+    accept_in,
+    current_in,
+    noise_in,
+    labels_in,
+    patch_in,
+    proj_in,
+    ada_in,
+    final_in,
+    time_in_ref,
+    time_out_ref,
+    qkv_ref,
+    out_ref,
+    state_ref,
+    error_ref,
     now_ref,
     step_ref,
     accept_ref,
@@ -91,12 +111,6 @@
     proj_ref,
     ada_ref,
     final_ref,
-    time_in_ref,
-    time_out_ref,
-    qkv_ref,
-    out_ref,
-    state_ref,
-    error_ref,
     time_in,
     time_out,
     wqkv,
@@ -111,6 +125,7 @@
     patch8,
     proj8,
     table,
+    unit,
     stream,
     normal,
     queries,
@@ -122,6 +137,7 @@
     probs,
     rows,
     local_sem,
+    small_sem,
     tile_sem,
     swap_sem,
     cond_sem,
@@ -139,24 +155,50 @@
     def own_row(pair):
         return jnp.where(side == 0, pair[0:1], pair[1:2])
 
-    barrier = pltpu.get_barrier_semaphore()
-    pl.semaphore_signal(barrier, inc=1, device_id=at(me, other), device_id_type=MESH)
-
-    along_x = [lax.rem(me + step, 4) for step in range(4)]
-    along_y = [lax.rem(me // 4 + step, 4) * 4 for step in range(4)]
-    along_z = [lax.rem(me // 16 + step, 4) * 16 for step in range(4)]
-    peers = [along_z[z] + along_y[y] + along_x[x] for z, y, x in OFFSETS]
-    for chip in peers:
-        pl.semaphore_signal(barrier, inc=1, device_id=at(chip, side), device_id_type=MESH)
-
     loads = [
         pltpu.make_async_copy(time_in_ref, time_in, local_sem.at[0]),
         pltpu.make_async_copy(time_out_ref, time_out, local_sem.at[1]),
         pltpu.make_async_copy(qkv_ref, wqkv.at[:, side], local_sem.at[2]),
         pltpu.make_async_copy(out_ref, wout.at[side], local_sem.at[3]),
     ]
-    for copy in loads:
+    for copy in loads[:2]:
         copy.start()
+    small = [
+        pltpu.make_async_copy(source, target, small_sem.at[slot])
+        for slot, (source, target) in enumerate(
+            (
+                (now_in, now_ref),
+                (step_in, step_ref),
+                (ada_in, ada_ref),
+                (final_in, final_ref),
+                (labels_in, labels_ref),
+                (current_in, current_ref),
+                (noise_in, noise_ref),
+                (patch_in, patch_ref),
+                (proj_in, proj_ref),
+                (accept_in, accept_ref),
+            )
+        )
+    ]
+    for copy in small:
+        copy.start()
+
+    barrier = pltpu.get_barrier_semaphore()
+    pl.semaphore_signal(barrier, inc=1, device_id=at(me, other), device_id_type=MESH)
+
+    along_x = [lax.rem(me + step, 4) for step in range(4)]
+    along_y = [lax.rem(me // 4 + step, 4) * 4 for step in range(4)]
+    along_z = [lax.rem(me // 16 + step, 4) * 16 for step in range(4)]
+    peers = [along_z[z] + along_y[y] + along_x[x] for z, y, x in OFFSETS]
+    holder = me < MOD_TILES
+
+    @pl.when(holder)
+    def _():
+        for chip in peers:
+            pl.semaphore_signal(barrier, inc=1, device_id=at(chip, side), device_id_type=MESH)
+
+    small[2].wait()
+    small[3].wait()
 
     def put(tile, values):
         for pair in range(9):
@@ -174,61 +216,70 @@
 
     @pl.when(side == 1)
     def _():
-        put(MOD_TILES, jnp.concatenate([blank, ada_ref[0, :, 0:64]], axis=1))
+        put(MOD_TILES - 1, jnp.concatenate([blank, ada_ref[0, :, 0:64]], axis=1))
         for tile in range(1, 14):
             start = tile * LANES - 64
             put(22 + tile, ada_ref[0, :, start : start + LANES])
         for tile in range(FEATURE_TILES):
             put(36 + tile, final_ref[:, tile * LANES : (tile + 1) * LANES])
 
+    for slot in (0, 1, 4):
+        small[slot].wait()
     time_now = jnp.full((1, LANES), now_ref[side], F32)
     step_size = jnp.full((1, LANES), step_ref[side], F32)
     later = time_now - step_size
     moments = jnp.concatenate([time_now, later, jnp.zeros((6, LANES), F32)], axis=0)
-    index = lanes_of((8, LANES)).astype(F32)
-    rates = jnp.exp(-math.log(10000.0) * index / (FREQ // 2))
-    angles = 1000.0 * moments * rates
-    features = jnp.concatenate([jnp.cos(angles), jnp.sin(angles)], axis=1).astype(BF16)
-    loads[0].wait()
-    hidden = silu(dot(features, time_in[...])).astype(BF16)
-    loads[1].wait()
-    both = labels_ref[...].astype(F32)
-    label = own_row(both)
-    cond = silu(label + dot(hidden, time_out[...])).astype(BF16)
-    for tile in range(FEATURE_TILES):
-        piece = cond[0:2, tile * LANES : (tile + 1) * LANES]
-        cond_send[tile] = piece
-        cond_all[tile, me] = piece
-
-    pl.semaphore_wait(barrier, CHIPS)
-
-    tile_swap = pltpu.make_async_remote_copy(
-        src_ref=stage.at[pl.ds(side * 23, 23)],
-        dst_ref=stage.at[pl.ds(side * 23, 23)],
-        send_sem=tile_sem.at[0],
-        recv_sem=tile_sem.at[1],
-        device_id=at(me, other),
-        device_id_type=MESH,
-    )
-    tile_swap.start()
+
+    def condition():
+        index = lanes_of((8, LANES)).astype(F32)
+        rates = jnp.exp(-math.log(10000.0) * index / (FREQ // 2))
+        angles = 1000.0 * moments * rates
+        features = jnp.concatenate([jnp.cos(angles), jnp.sin(angles)], axis=1).astype(BF16)
+        loads[0].wait()
+        hidden = silu(dot(features, time_in[...])).astype(BF16)
+        loads[1].wait()
+        loads[2].start()
+        loads[3].start()
+        label = own_row(labels_ref[...].astype(F32))
+        cond = silu(label + dot(hidden, time_out[...])).astype(BF16)
+        for tile in range(FEATURE_TILES):
+            piece = cond[0:2, tile * LANES : (tile + 1) * LANES]
+            cond_send[tile] = piece
+            cond_all[tile, me] = piece
+
+    early = me < CHIPS // 2
+    pl.when(early)(condition)
+
+    @pl.when(holder)
+    def _():
+        pl.semaphore_wait(barrier, MOD_TILES)
+
+    @pl.when(jnp.logical_not(holder))
+    def _():
+        pl.semaphore_wait(barrier, MOD_TILES + 1)
+
+    pl.when(jnp.logical_not(early))(condition)
 
     for chip in peers:
-        pltpu.make_async_remote_copy(
-            src_ref=cond_send,
-            dst_ref=cond_all.at[:, me],
-            send_sem=cond_sem.at[0],
-            recv_sem=cond_sem.at[1],
-            device_id=at(chip, side),
-            device_id_type=MESH,
-        ).start()
-
-    tile_swap.wait()
-    for pair in range(9):
-        stage[13, pair] = stage[13, pair] + stage[MOD_TILES, pair]
-
+
+        @pl.when(chip < MOD_TILES)
+        def _():
+            pltpu.make_async_remote_copy(
+                src_ref=cond_send,
+                dst_ref=cond_all.at[:, me],
+                send_sem=cond_sem.at[0],
+                recv_sem=cond_sem.at[1],
+                device_id=at(chip, side),
+                device_id_type=MESH,
+            ).start()
+
+    def ours(chip):
+        return jnp.logical_and(chip < MOD_TILES, (chip < SIDE_TILES) == (side == 0))
+
+    direct = ours(me)
     for chip in peers:
 
-        @pl.when(chip < MOD_TILES)
+        @pl.when(ours(chip))
         def _():
             pltpu.make_async_remote_copy(
                 src_ref=stage.at[chip],
@@ -239,9 +290,18 @@
                 device_id_type=MESH,
             ).start()
 
-    @pl.when(me < MOD_TILES)
+    @pl.when(direct)
     def _():
         tiles_all[pl.ds(me * 9, 9)] = stage[me]
+
+    tile_share = pltpu.make_async_remote_copy(
+        src_ref=tiles_all,
+        dst_ref=tiles_all,
+        send_sem=tile_sem.at[0],
+        recv_sem=tile_sem.at[1],
+        device_id=at(me, other),
+        device_id_type=MESH,
+    )
 
     swaps = []
     for slot, (src, dst) in enumerate(((qkv_ref, wqkv.at[:, side]), (out_ref, wout.at[side]))):
@@ -257,6 +317,8 @@
         )
         swaps[-1].start()
 
+    for copy in small[5:]:
+        copy.wait()
     lane8 = lanes_of((CHUNK_ROWS, LANES)) // PATCH_VALS
     for piece in range(CHUNK_ROWS):
         span = slice(piece * LANES, (piece + 1) * LANES)
@@ -286,14 +348,39 @@
 
     lax.fori_loop(0, PER_ROW, table_chunk, 0)
 
+    spans = [slice(j * CHUNK_ROWS, (j + 1) * CHUNK_ROWS) for j in range(PER_ROW)]
+
+    def prepare(latent):
+        tokens = jnp.concatenate(
+            [jnp.where(lane8 == j, latent, 0.0) for j in range(PER_ROW)], axis=0
+        ).astype(BF16)
+        stream[...] = dot(tokens, patch8[...]) + table[...]
+        means, spreads = moments_of(stream, spans)
+        for span, mean, scale in zip(spans, means, spreads):
+            unit[span] = (stream[span] - mean) * scale
+
+    prepare(current)
+
     def drain(ref, sem):
         pltpu.make_async_copy(ref, ref, sem).wait()
 
-    drain(cond_all.at[:, pl.ds(0, CHIPS - 1)], cond_sem.at[1])
-
-    @pl.when(me < MOD_TILES)
+    relay = jnp.logical_and(holder, jnp.logical_not(direct))
+
+    @pl.when(direct)
     def _():
         drain(tiles_all.at[pl.ds(0, 9 * (CHIPS - 1))], weight_sem.at[1])
+        tile_share.start()
+
+    @pl.when(holder)
+    def _():
+        drain(cond_all.at[:, pl.ds(0, CHIPS - 1)], cond_sem.at[1])
+
+    @pl.when(relay)
+    def _():
+        tile_share.wait_recv()
+
+    @pl.when(holder)
+    def _():
         total = jnp.zeros((2 * CHIPS, LANES), F32)
         for tile in range(FEATURE_TILES):
             lhs = cond_all[tile].reshape(2 * CHIPS, LANES)
@@ -312,7 +399,7 @@
                 device_id_type=MESH,
             ).start()
 
-    @pl.when(me < MOD_TILES)
+    @pl.when(holder)
     def _():
         drain(mods.at[pl.ds(0, MOD_TILES - 1)], mod_sem.at[1])
 
@@ -326,21 +413,16 @@
         swap.wait()
 
     def mod_row(which, moment):
-        tiles = [mods[chip] for chip in TILE_CHIPS[which]]
+        tiles = [mods[chip] + mods[45] if chip == 13 else mods[chip] for chip in TILE_CHIPS[which]]
         pair = jnp.concatenate(tiles, axis=1)
         return jnp.where(moment == 0, pair[0:1], pair[1:2])
 
     exponent = HEAD_DIM ** (-0.5) * math.log2(math.e)
 
-    def evaluate(latent, moment):
-        tokens = jnp.concatenate(
-            [jnp.where(lane8 == j, latent, 0.0) for j in range(PER_ROW)], axis=0
-        ).astype(BF16)
-        stream[...] = dot(tokens, patch8[...]) + table[...]
+    def evaluate(moment):
         shift, scale = mod_row(0, moment), 1.0 + mod_row(1, moment)
-        for j in range(PER_ROW):
-            span = slice(j * CHUNK_ROWS, (j + 1) * CHUNK_ROWS)
-            normal[span] = (normed(stream[span]) * scale + shift).astype(BF16)
+        for span in spans:
+            normal[span] = (unit[span] * scale + shift).astype(BF16)
 
         turned[...] = normal[...].T
         weight = [wqkv[part].reshape(D, D) for part in range(3)]
@@ -388,9 +470,9 @@
         )
         stream[...] = stream[...] + mod_row(2, moment) * attended
         shift, scale = mod_row(3, moment), 1.0 + mod_row(4, moment)
-        for j in range(PER_ROW):
-            span = slice(j * CHUNK_ROWS, (j + 1) * CHUNK_ROWS)
-            normal[span] = (normed(stream[span]) * scale + shift).astype(BF16)
+        means, spreads = moments_of(stream, spans)
+        for span, mean, spread_inv in zip(spans, means, spreads):
+            normal[span] = ((stream[span] - mean) * spread_inv * scale + shift).astype(BF16)
         guessed = dot_t(normal[...], proj8[...])
         result = jnp.zeros((CHUNK_ROWS, LANES), F32)
         for j in range(PER_ROW):
@@ -401,10 +483,9 @@
 
     spread = jnp.sqrt(step_size * beta_at(time_now)) * draw
 
-    rows[2] = current
 
     def one_moment(moment, carry):
-        guess = evaluate(rows[2], moment)
+        guess = evaluate(moment)
         rows[4] = guess
 
         @pl.when(moment == 0)
@@ -412,7 +493,9 @@
             rows[3] = guess
             beta = beta_at(time_now)
             drift_now = 0.5 * beta * rows[0] - beta * guess / sigma_at(time_now)
-            rows[2] = rows[0] + step_size * drift_now + spread
+            euler_now = rows[0] + step_size * drift_now + spread
+            rows[2] = euler_now
+            prepare(euler_now)
 
         return carry
 
@@ -442,15 +525,23 @@
     )
     final_swap.start()
 
-    drain(cond_all.at[:, pl.ds(0, CHIPS - 1)], cond_sem.at[0])
     @pl.when(me >= MOD_TILES)
     def _():
-        drain(tiles_all.at[pl.ds(0, 9 * MOD_TILES)], weight_sem.at[0])
+        drain(cond_all.at[:, pl.ds(0, MOD_TILES)], cond_sem.at[0])
 
     @pl.when(me < MOD_TILES)
     def _():
-        drain(tiles_all.at[pl.ds(0, 9 * (MOD_TILES - 1))], weight_sem.at[0])
+        drain(cond_all.at[:, pl.ds(0, MOD_TILES - 1)], cond_sem.at[0])
         drain(mod_send.at[pl.ds(0, CHIPS - 1)], mod_sem.at[0])
+
+    @pl.when(direct)
+    def _():
+        drain(tiles_all.at[pl.ds(0, 9 * (SIDE_TILES - 1))], weight_sem.at[0])
+        tile_share.wait_send()
+
+    @pl.when(jnp.logical_not(direct))
+    def _():
+        drain(tiles_all.at[pl.ds(0, 9 * SIDE_TILES)], weight_sem.at[0])
 
     final_swap.wait()
     for latent in range(2):
@@ -477,23 +568,32 @@
     final_ada,
     final_proj,
 ):
-    smem = pl.BlockSpec(memory_space=pltpu.SMEM)
     vmem = pl.BlockSpec(memory_space=pltpu.VMEM)
     place = pl.BlockSpec(memory_space=pl.ANY)
     state, error = pl.pallas_call(
         kernel,
         out_shape=(
-            jax.ShapeDtypeStruct((2, LATENT), F32),
-            jax.ShapeDtypeStruct((2, LANES), F32),
+            pltpu.VMEM((2, LATENT), F32),
+            pltpu.VMEM((2, LANES), F32),
         ),
-        in_specs=[smem] * 3 + [vmem] * 7 + [place] * 4,
+        in_specs=[place] * 14,
         out_specs=(vmem, vmem),
         scratch_shapes=[
+            pltpu.SMEM((2,), F32),
+            pltpu.SMEM((2,), F32),
+            pltpu.SMEM((2,), jnp.int32),
+            pltpu.VMEM((2, LATENT), F32),
+            pltpu.VMEM((2, LATENT), F32),
+            pltpu.VMEM((2, D), BF16),
+            pltpu.VMEM((PATCH_VALS, D), BF16),
+            pltpu.VMEM((PATCH_VALS, D), BF16),
+            pltpu.VMEM((1, 18, 3 * HALF), BF16),
+            pltpu.VMEM((18, D), BF16),
             pltpu.VMEM((FREQ, D), BF16),
             pltpu.VMEM((D, D), BF16),
             pltpu.VMEM((3, GROUPS, HALF, D), BF16),
             pltpu.VMEM((GROUPS, HALF, D), BF16),
-            pltpu.VMEM((MOD_TILES + 1, 9, 2, LANES), BF16),
+            pltpu.VMEM((MOD_TILES, 9, 2, LANES), BF16),
             pltpu.VMEM((FEATURE_TILES, 2, LANES), BF16),
             pltpu.VMEM((FEATURE_TILES, CHIPS, 2, LANES), BF16),
             pltpu.VMEM((9 * CHIPS, 2, LANES), BF16),
@@ -502,6 +602,7 @@
             pltpu.VMEM((2, CHUNK_ROWS + 8, LANES), F32),
             pltpu.VMEM((LANES, D), BF16),
             pltpu.VMEM((LANES, D), BF16),
+            pltpu.VMEM((TOK, D), F32),
             pltpu.VMEM((TOK, D), F32),
             pltpu.VMEM((TOK, D), F32),
             pltpu.VMEM((TOK, D), BF16),
@@ -514,6 +615,7 @@
             pltpu.VMEM((2, TOK, TOK), BF16),
             pltpu.VMEM((5, CHUNK_ROWS, LANES), F32),
             pltpu.SemaphoreType.DMA((4,)),
+            pltpu.SemaphoreType.DMA((10,)),
             pltpu.SemaphoreType.DMA((2,)),
             pltpu.SemaphoreType.DMA((4,)),
             pltpu.SemaphoreType.DMA((2,)),

time: 45 us -> 41 us (0.911)
  Pallas kernels: 41.5 us -> 39 us
  local copies, waits for them, and re-layouts: 2.65 us -> 1.24 us
    pallas_call x1, Pallas kernels: 41.5 us -> 39 us  [shards(): pl.pallas_call(kernel, out_shape=(pltpu.VMEM((2, LATENT), F32), pltpu.VME...]
    unnamed x1, local copies, waits for them, and re-layouts: 1.37 us -> 0.62 us
    slice x1, local copies, waits for them, and re-layouts: 1.28 us -> 0.63 us  [shards(): return (state, error[:, 0])]
where the time goes in v3:
time: 41 us; the launch traced here: 40.8 us
  Pallas kernels  39 us (95%)
  local copies, waits for them, and re-layouts  1.24 us (3%)
  between operations  0.64 us (2%)
    pallas_call x1, Pallas kernels, shards(): pl.pallas_call(kernel, out_shape=(pltpu.VMEM((2, LATENT), F32), pltpu.VME...  39 us

profile of v3, /device:TPU:1, one launch (start us, length us, event | category | flops | bytes accessed | tf_op | source)
XLA Modules:
  0.0 40.8 jit_solution(4579458736740940049)
XLA Ops:
  0.6 39.0 %heun_step.1 = (f32[2,4096]{1,0:T(2,128)S(1)}, f32[2,128]{1,0:T(2,128)S(1)}) custom-call(f32[2]{0:T(128)} %now_in.1, f32[2]{0:T(128)} %step_in.1, s32[2]{0:T(128)} %accept_in.1, f32[2,4096]{1,0:T(2,128)} %current_in.1, f32[2,4096]{1,0:T(2,128)} %noise_in.1, bf16[2,1152]{1,0:T(2,128)(2,1)} %labels_in.1, bf16[16,1152]{1,0:T(8,128)(2,1)} %patch_in.1, ...), custom_call_target="tpu_custom_call" | custom-call | tf_op jit(solution)/shard_map/heun_step/pallas_call | solution.py:573
  39.6 0.6 %copy.17 = f32[2,4096]{1,0:T(2,128)} copy(f32[2,4096]{1,0:T(2,128)S(1)} %get-tuple-element.6) | data formatting | bytes 65536
  40.2 0.6 %slice_reduce_fusion = f32[2]{0:T(128)} fusion(f32[2,128]{1,0:T(2,128)S(1)} %get-tuple-element.5), kind=kLoop, calls=%fused_computation | loop fusion | bytes 16 | tf_op jit(solution)/shard_map/slice | solution.py:646

commit v4 on v3

--- a/solution.py
+++ b/solution.py
@@ -21,6 +21,7 @@
 LATENT = 4096
 GROUPS = 2
 HALF = D // GROUPS
+FOUR = 4 * HEAD_DIM
 LANES = 128
 CHUNK_ROWS = LATENT // LANES
 PER_ROW = LANES // PATCH_VALS
@@ -155,11 +156,12 @@
     def own_row(pair):
         return jnp.where(side == 0, pair[0:1], pair[1:2])
 
+    own_half = pl.ds(pl.multiple_of(side * HALF, HALF), HALF)
     loads = [
         pltpu.make_async_copy(time_in_ref, time_in, local_sem.at[0]),
         pltpu.make_async_copy(time_out_ref, time_out, local_sem.at[1]),
         pltpu.make_async_copy(qkv_ref, wqkv.at[:, side], local_sem.at[2]),
-        pltpu.make_async_copy(out_ref, wout.at[side], local_sem.at[3]),
+        pltpu.make_async_copy(out_ref, wout.at[own_half], local_sem.at[3]),
     ]
     for copy in loads[:2]:
         copy.start()
@@ -245,7 +247,7 @@
         for tile in range(FEATURE_TILES):
             piece = cond[0:2, tile * LANES : (tile + 1) * LANES]
             cond_send[tile] = piece
-            cond_all[tile, me] = piece
+            cond_all[me, tile] = piece
 
     early = me < CHIPS // 2
     pl.when(early)(condition)
@@ -258,41 +260,49 @@
     def _():
         pl.semaphore_wait(barrier, MOD_TILES + 1)
 
+    base = side * SIDE_TILES
+    direct = jnp.logical_and(me >= base, me < base + SIDE_TILES)
+
+    def send_tile(step):
+        chip = base + lax.rem(me + step, SIDE_TILES)
+        pltpu.make_async_remote_copy(
+            src_ref=stage.at[chip],
+            dst_ref=tiles_all.at[pl.ds(me * 9, 9)],
+            send_sem=weight_sem.at[0],
+            recv_sem=weight_sem.at[1],
+            device_id=at(chip, side),
+            device_id_type=MESH,
+        ).start()
+
+    def send_rows(step):
+        pltpu.make_async_remote_copy(
+            src_ref=cond_send,
+            dst_ref=cond_all.at[me],
+            send_sem=cond_sem.at[0],
+            recv_sem=cond_sem.at[1],
+            device_id=at(lax.rem(me + step, MOD_TILES), side),
+            device_id_type=MESH,
+        ).start()
+
+    for step in range(1, SIDE_TILES):
+        send_tile(step)
+
+    @pl.when(jnp.logical_not(direct))
+    def _():
+        send_tile(0)
+
+    @pl.when(direct)
+    def _():
+        tiles_all[pl.ds(me * 9, 9)] = stage[me]
+
     pl.when(jnp.logical_not(early))(condition)
 
-    for chip in peers:
-
-        @pl.when(chip < MOD_TILES)
-        def _():
-            pltpu.make_async_remote_copy(
-                src_ref=cond_send,
-                dst_ref=cond_all.at[:, me],
-                send_sem=cond_sem.at[0],
-                recv_sem=cond_sem.at[1],
-                device_id=at(chip, side),
-                device_id_type=MESH,
-            ).start()
-
-    def ours(chip):
-        return jnp.logical_and(chip < MOD_TILES, (chip < SIDE_TILES) == (side == 0))
-
-    direct = ours(me)
-    for chip in peers:
-
-        @pl.when(ours(chip))
-        def _():
-            pltpu.make_async_remote_copy(
-                src_ref=stage.at[chip],
-                dst_ref=tiles_all.at[pl.ds(me * 9, 9)],
-                send_sem=weight_sem.at[0],
-                recv_sem=weight_sem.at[1],
-                device_id=at(chip, side),
-                device_id_type=MESH,
-            ).start()
-
-    @pl.when(direct)
-    def _():
-        tiles_all[pl.ds(me * 9, 9)] = stage[me]
+    for step in range(1, MOD_TILES):
+        send_rows(step)
+
+    @pl.when(jnp.logical_not(holder))
+    def _():
+        send_rows(0)
 
     tile_share = pltpu.make_async_remote_copy(
         src_ref=tiles_all,
@@ -304,7 +314,7 @@
     )
 
     swaps = []
-    for slot, (src, dst) in enumerate(((qkv_ref, wqkv.at[:, side]), (out_ref, wout.at[side]))):
+    for slot, (src, dst) in enumerate(((qkv_ref, wqkv.at[:, side]), (out_ref, wout.at[own_half]))):
         swaps.append(
             pltpu.make_async_remote_copy(
                 src_ref=src,
@@ -335,6 +345,8 @@
     proj8[...] = dot(jnp.where(spread_lanes, 1.0, 0.0).astype(BF16), proj_ref[...]).astype(BF16)
 
     half = D // 2
+    queries[...] = jnp.zeros_like(queries)
+
     def table_chunk(j, carry):
         place = lax.broadcasted_iota(jnp.int32, (CHUNK_ROWS, D), 0) * PER_ROW + j
         column = lanes_of((CHUNK_ROWS, D))
@@ -373,7 +385,7 @@
 
     @pl.when(holder)
     def _():
-        drain(cond_all.at[:, pl.ds(0, CHIPS - 1)], cond_sem.at[1])
+        drain(cond_all.at[pl.ds(0, CHIPS - 1)], cond_sem.at[1])
 
     @pl.when(relay)
     def _():
@@ -383,7 +395,7 @@
     def _():
         total = jnp.zeros((2 * CHIPS, LANES), F32)
         for tile in range(FEATURE_TILES):
-            lhs = cond_all[tile].reshape(2 * CHIPS, LANES)
+            lhs = cond_all[:, tile].reshape(2 * CHIPS, LANES)
             rhs = tiles_all[tile * 64 : (tile + 1) * 64].reshape(LANES, LANES)
             total = total + dot(lhs, rhs)
         mod_send[...] = total.reshape(CHIPS, 2, LANES)
@@ -417,6 +429,7 @@
         pair = jnp.concatenate(tiles, axis=1)
         return jnp.where(moment == 0, pair[0:1], pair[1:2])
 
+    nothing = jnp.zeros((8, TOK), F32)
     exponent = HEAD_DIM ** (-0.5) * math.log2(math.e)
 
     def evaluate(moment):
@@ -425,50 +438,58 @@
             normal[span] = (unit[span] * scale + shift).astype(BF16)
 
         turned[...] = normal[...].T
-        weight = [wqkv[part].reshape(D, D) for part in range(3)]
-        queries[...] = (dot(weight[0], turned[...]) * exponent).astype(BF16)
-        keys[...] = dot(weight[1], turned[...]).astype(BF16).T
-        values[...] = dot(weight[2], turned[...]).astype(BF16)
+        keys[...] = dot(wqkv[1].reshape(D, D), turned[...]).astype(BF16).T
+
+        def project(four):
+            group, row = four // 2, four % 2 * FOUR
+            asked = dot(wqkv[0, group, row : row + FOUR], turned[...]) * exponent
+            given = dot(wqkv[2, group, row : row + FOUR], turned[...])
+            for place in range(4):
+                head = 4 * four + place
+                low = head * HEAD_DIM
+                span = slice(place * HEAD_DIM, (place + 1) * HEAD_DIM)
+                rows72 = [asked[span], nothing] if low % 16 == 0 else [nothing, asked[span]]
+                start = low // 16 * 16 - low // LANES * LANES
+                queries[head, start : start + 80] = jnp.concatenate(rows72, axis=0).astype(BF16)
+                values[head] = jnp.concatenate([given[span], nothing + 1.0], axis=0).astype(BF16)
+
+        def leave():
+            return lax.dot_general(
+                mixed[...].astype(BF16),
+                wout[...],
+                (((0,), (0,)), ((), ())),
+                preferred_element_type=F32,
+            )
 
         def score(head):
             low, high = head * HEAD_DIM, (head + 1) * HEAD_DIM
             left = low // LANES * LANES
             right = -(-high // LANES) * LANES
-            row = lax.broadcasted_iota(jnp.int32, (right - left, 1), 0) + left
-            asked = queries[left:right]
-            asked = jnp.where((row >= low) & (row < high), asked, jnp.zeros_like(asked))
-            scores[head % 2] = dot(keys[:, left:right], asked)
+            scores[head % 2] = dot(keys[:, left:right], queries[head, : right - left])
 
         def soften(head):
             found = scores[head % 2]
             weights = jnp.exp2(found - jnp.max(found, axis=0, keepdims=True))
             probs[head % 2] = weights.astype(BF16)
-            return jnp.sum(weights, axis=0, keepdims=True)
-
-        def apply(head, whole):
-            low, high = head * HEAD_DIM, (head + 1) * HEAD_DIM
-            first = low // 16 * 16
-            result = dot(values[first : first + 80], probs[head % 2])
-            mixed[low:high] = result[low - first : high - first] * (1.0 / whole)
-
+
+        def apply(head):
+            result = dot(values[head], probs[head % 2])
+            mixed[head * HEAD_DIM : (head + 1) * HEAD_DIM] = result[:HEAD_DIM] * (
+                1.0 / result[HEAD_DIM : HEAD_DIM + 1]
+            )
+
+        project(0)
         score(0)
-        before = None
         for head in range(HEADS):
+            if head % 4 == 0 and head + 4 < HEADS:
+                project(head // 4 + 1)
             if head + 1 < HEADS:
                 score(head + 1)
-            whole = soften(head)
+            soften(head)
             if head:
-                apply(head - 1, before)
-            before = whole
-        apply(HEADS - 1, before)
-
-        attended = lax.dot_general(
-            mixed[...].astype(BF16),
-            wout[...].reshape(D, D),
-            (((0,), (0,)), ((), ())),
-            preferred_element_type=F32,
-        )
-        stream[...] = stream[...] + mod_row(2, moment) * attended
+                apply(head - 1)
+        apply(HEADS - 1)
+        stream[...] = stream[...] + mod_row(2, moment) * leave()
         shift, scale = mod_row(3, moment), 1.0 + mod_row(4, moment)
         means, spreads = moments_of(stream, spans)
         for span, mean, spread_inv in zip(spans, means, spreads):
@@ -527,11 +548,11 @@
 
     @pl.when(me >= MOD_TILES)
     def _():
-        drain(cond_all.at[:, pl.ds(0, MOD_TILES)], cond_sem.at[0])
+        drain(cond_all.at[pl.ds(0, MOD_TILES)], cond_sem.at[0])
 
     @pl.when(me < MOD_TILES)
     def _():
-        drain(cond_all.at[:, pl.ds(0, MOD_TILES - 1)], cond_sem.at[0])
+        drain(cond_all.at[pl.ds(0, MOD_TILES - 1)], cond_sem.at[0])
         drain(mod_send.at[pl.ds(0, CHIPS - 1)], mod_sem.at[0])
 
     @pl.when(direct)
@@ -592,10 +613,10 @@
             pltpu.VMEM((FREQ, D), BF16),
             pltpu.VMEM((D, D), BF16),
             pltpu.VMEM((3, GROUPS, HALF, D), BF16),
-            pltpu.VMEM((GROUPS, HALF, D), BF16),
+            pltpu.VMEM((D, D), BF16),
             pltpu.VMEM((MOD_TILES, 9, 2, LANES), BF16),
             pltpu.VMEM((FEATURE_TILES, 2, LANES), BF16),
-            pltpu.VMEM((FEATURE_TILES, CHIPS, 2, LANES), BF16),
+            pltpu.VMEM((CHIPS, FEATURE_TILES, 2, LANES), BF16),
             pltpu.VMEM((9 * CHIPS, 2, LANES), BF16),
             pltpu.VMEM((CHIPS, 2, LANES), F32),
             pltpu.VMEM((MOD_TILES, 2, LANES), F32),
@@ -606,9 +627,9 @@
             pltpu.VMEM((TOK, D), F32),
             pltpu.VMEM((TOK, D), F32),
             pltpu.VMEM((TOK, D), BF16),
-            pltpu.VMEM((D, TOK), BF16),
+            pltpu.VMEM((HEADS, 2 * LANES, TOK), BF16),
             pltpu.VMEM((TOK, D), BF16),
-            pltpu.VMEM((D, TOK), BF16),
+            pltpu.VMEM((HEADS, 80, TOK), BF16),
             pltpu.VMEM((D, TOK), F32),
             pltpu.VMEM((D, TOK), BF16),
             pltpu.VMEM((2, TOK, TOK), F32),

time: 41 us -> 40.3 us (0.983)
  Pallas kernels: 39 us -> 38.3 us
    pallas_call x1, Pallas kernels: 39 us -> 38.3 us  [shards(): pl.pallas_call(kernel, out_shape=(pltpu.VMEM((2, LATENT), F32), pltpu.VME...]
where the time goes in v4:
time: 40.3 us; the launch traced here: 40.2 us
  Pallas kernels  38.3 us (95%)
  local copies, waits for them, and re-layouts  1.24 us (3%)
  between operations  0.64 us (2%)
    pallas_call x1, Pallas kernels, shards(): pl.pallas_call(kernel, out_shape=(pltpu.VMEM((2, LATENT), F32), pltpu.VME...  38.3 us

profile of v4, /device:TPU:1, one launch (start us, length us, event | category | flops | bytes accessed | tf_op | source)
XLA Modules:
  0.0 40.2 jit_solution(4293143424630102489)
XLA Ops:
  0.6 38.3 %heun_step.1 = (f32[2,4096]{1,0:T(2,128)S(1)}, f32[2,128]{1,0:T(2,128)S(1)}) custom-call(f32[2]{0:T(128)} %now_in.1, f32[2]{0:T(128)} %step_in.1, s32[2]{0:T(128)} %accept_in.1, f32[2,4096]{1,0:T(2,128)} %current_in.1, f32[2,4096]{1,0:T(2,128)} %noise_in.1, bf16[2,1152]{1,0:T(2,128)(2,1)} %labels_in.1, bf16[16,1152]{1,0:T(8,128)(2,1)} %patch_in.1, ...), custom_call_target="tpu_custom_call" | custom-call | tf_op jit(solution)/shard_map/heun_step/pallas_call | solution.py:594
  38.9 0.6 %copy.17 = f32[2,4096]{1,0:T(2,128)} copy(f32[2,4096]{1,0:T(2,128)S(1)} %get-tuple-element.6) | data formatting | bytes 65536
  39.5 0.6 %slice_reduce_fusion = f32[2]{0:T(128)} fusion(f32[2,128]{1,0:T(2,128)S(1)} %get-tuple-element.5), kind=kLoop, calls=%fused_computation | loop fusion | bytes 16 | tf_op jit(solution)/shard_map/slice | solution.py:667

commit v5 on v4

--- a/solution.py
+++ b/solution.py
@@ -570,7 +570,12 @@
             state_ref[latent : latent + 1, piece * LANES : (piece + 1) * LANES] = finals[
                 latent, piece : piece + 1, :
             ]
-        error_ref[latent : latent + 1, :] = finals[latent, CHUNK_ROWS : CHUNK_ROWS + 1, :]
+    pair = jnp.where(
+        lanes_of((1, LANES)) == 0,
+        finals[0, CHUNK_ROWS : CHUNK_ROWS + 1, :],
+        finals[1, CHUNK_ROWS : CHUNK_ROWS + 1, :],
+    )
+    error_ref[...] = pair[0, :2]
 
 
 def shards(
@@ -595,7 +600,7 @@
         kernel,
         out_shape=(
             pltpu.VMEM((2, LATENT), F32),
-            pltpu.VMEM((2, LANES), F32),
+            pltpu.VMEM((2,), F32),
         ),
         in_specs=[place] * 14,
         out_specs=(vmem, vmem),
@@ -664,7 +669,7 @@
         qkv_weight[0].transpose(1, 2, 0),
         out_weight[0].T,
     )
-    return state, error[:, 0]
+    return state, error
 
 
 def solution(mesh):

time: 40.3 us -> 40.2 us (level)
    slice x1 -> x0, local copies, waits for them, and re-layouts: 0.63 us -> none  [shards(): return (state, error[:, 0])]
    unnamed x1 -> x2, local copies, waits for them, and re-layouts: 0.62 us -> 1.13 us
where the time goes in v5:
time: 40.2 us; the launch traced here: 40.1 us
  Pallas kernels  38.3 us (95%)
  local copies, waits for them, and re-layouts  1.13 us (3%)
  between operations  0.64 us (2%)
    pallas_call x1, Pallas kernels, shards(): pl.pallas_call(kernel, out_shape=(pltpu.VMEM((2, LATENT), F32), pltpu.VME...  38.3 us
    unnamed x2, local copies, waits for them, and re-layouts  1.13 us

profile of v5, /device:TPU:1, one launch (start us, length us, event | category | flops | bytes accessed | tf_op | source)
XLA Modules:
  0.0 40.1 jit_solution(3229929408332466170)
XLA Ops:
  0.6 38.3 %heun_step.1 = (f32[2,4096]{1,0:T(2,128)S(1)}, f32[2]{0:T(128)S(1)}) custom-call(f32[2]{0:T(128)} %now_in.1, f32[2]{0:T(128)} %step_in.1, s32[2]{0:T(128)} %accept_in.1, f32[2,4096]{1,0:T(2,128)} %current_in.1, f32[2,4096]{1,0:T(2,128)} %noise_in.1, bf16[2,1152]{1,0:T(2,128)(2,1)} %labels_in.1, bf16[16,1152]{1,0:T(8,128)(2,1)} %patch_in.1, ...), custom_call_target="tpu_custom_call" | custom-call | tf_op jit(solution)/shard_map/heun_step/pallas_call | solution.py:599
  38.9 0.6 %copy.18 = f32[2,4096]{1,0:T(2,128)} copy(f32[2,4096]{1,0:T(2,128)S(1)} %get-tuple-element.2) | data formatting | bytes 65536
  39.5 0.5 %copy.19 = f32[2]{0:T(128)} copy(f32[2]{0:T(128)S(1)} %get-tuple-element.3) | data formatting | bytes 16
